TPU v7x, 16 devices: a 4x2x1 block of a 4x4x8 slice. The times are simulated.
16 devices in a mesh: dp: 2 (over y, z), tp: 8 (over x, core).
Axes of the slice: x: 4, y: 2, z: 1, core: 2. Of those that a mesh axis runs over, the one named last changes fastest.
The devices are a block of a 4x4x8 slice.
Arguments:
- hidden: bfloat16 [2048, 2048], P('dp'), parts along dimension 0
- w_q: bfloat16 [2048, 2048], P(None, 'tp')
- w_k: bfloat16 [2048, 2048], P(None, 'tp')
- w_v: bfloat16 [2048, 2048], P(None, 'tp')
- w_o: bfloat16 [2048, 2048], P('tp')
- q_norm_w: float32 [2048], P('tp')
- k_norm_w: float32 [2048], P('tp')
- post_norm_w: float32 [2048], replicated
- k_cache: bfloat16 [2048, 32, 16, 128], P('dp', None, 'tp'), parts along dimension 0
- v_cache: bfloat16 [2048, 32, 16, 128], P('dp', None, 'tp'), parts along dimension 0
- positions: int32 [2048], P('dp'), parts along dimension 0
Outputs:
- output 1: bfloat16 [2048, 2048], P('dp'), parts along dimension 0
- output 2: bfloat16 [2048, 32, 16, 128], P('dp', None, 'tp'), parts along dimension 0
- output 3: bfloat16 [2048, 32, 16, 128], P('dp', None, 'tp'), parts along dimension 0
There are 2 independent parts. A program takes and returns all parts, laid end to end along the dimension named above; an argument that names none is the same for every part.
All inputs are finite; a program needn't handle non-finite values.
Results may differ from a plain program's by a relative error of at most 0.0111559.
Values are sent between devices in bfloat16 or wider.
A program may use at most 768 MiB of HBM per device.

v0:
```python
import jax
import jax.numpy as jnp
from jax import lax
from jax.sharding import PartitionSpec as P

NORM_EPS = 1e-6
ROPE_BASE = 500000.0


def apply_rope(heads_val, positions):
    head_dim = heads_val.shape[-1]
    half = head_dim // 2
    inv_freq = ROPE_BASE ** (-2.0 * jnp.arange(half, dtype=jnp.float32) / head_dim)
    angles = positions.astype(jnp.float32)[:, None, None] * inv_freq[None, None, :]
    cos_tab = jnp.cos(angles)
    sin_tab = jnp.sin(angles)
    wide = heads_val.astype(jnp.float32)
    first = wide[..., :half]
    second = wide[..., half:]
    return jnp.concatenate([first * cos_tab - second * sin_tab, second * cos_tab + first * sin_tab], axis=-1).astype(jnp.bfloat16)


def write_slot(cache, new_vals, positions):
    slot_ids = jnp.arange(cache.shape[1], dtype=jnp.int32)
    at_slot = (slot_ids[None, :] == positions[:, None])[:, :, None, None]
    return jnp.where(at_slot, new_vals[:, None], cache)


def attend(q_rot, k_new, v_new, positions):
    slot_ids = jnp.arange(k_new.shape[1], dtype=jnp.int32)
    scores = jnp.einsum('bhd,bshd->bhs', q_rot, k_new, preferred_element_type=jnp.float32) * k_new.shape[3] ** -0.5
    valid = (slot_ids[None, :] <= positions[:, None])[:, None, :]
    scores = jnp.where(valid, scores, -1e30)
    probs = jax.nn.softmax(scores, axis=-1).astype(jnp.bfloat16)
    return jnp.einsum('bhs,bshd->bhd', probs, v_new, preferred_element_type=jnp.float32).astype(jnp.bfloat16)


def solution(mesh):
    def local_step(hidden, w_q, w_k, w_v, w_o, q_norm_w, k_norm_w, post_norm_w, k_cache, v_cache, positions):
        n_rows, width = hidden.shape
        local_heads, head_dim = k_cache.shape[2], k_cache.shape[3]
        q_local = jnp.dot(hidden, w_q, preferred_element_type=jnp.float32).astype(jnp.bfloat16).astype(jnp.float32)
        k_local = jnp.dot(hidden, w_k, preferred_element_type=jnp.float32).astype(jnp.bfloat16).astype(jnp.float32)
        v_local = jnp.dot(hidden, w_v, preferred_element_type=jnp.float32).astype(jnp.bfloat16)
        energy = jnp.stack([jnp.sum(q_local * q_local, axis=-1), jnp.sum(k_local * k_local, axis=-1)])
        energy = lax.psum(energy, 'tp')
        inv_rms = lax.rsqrt(energy / width + NORM_EPS)
        q_normed = (q_local * inv_rms[0][:, None] * q_norm_w).astype(jnp.bfloat16).reshape(n_rows, local_heads, head_dim)
        k_normed = (k_local * inv_rms[1][:, None] * k_norm_w).astype(jnp.bfloat16).reshape(n_rows, local_heads, head_dim)
        q_rot = apply_rope(q_normed, positions)
        k_rot = apply_rope(k_normed, positions)
        k_new = write_slot(k_cache, k_rot, positions)
        v_new = write_slot(v_cache, v_local.reshape(n_rows, local_heads, head_dim), positions)
        attn = attend(q_rot, k_new, v_new, positions)
        proj_part = jnp.dot(attn.reshape(n_rows, local_heads * head_dim), w_o, preferred_element_type=jnp.float32).astype(jnp.bfloat16)
        a_out = lax.psum(proj_part, 'tp').astype(jnp.float32)
        inv_out = lax.rsqrt(jnp.mean(a_out * a_out, axis=-1, keepdims=True) + NORM_EPS)
        hidden_out = (hidden.astype(jnp.float32) + a_out * inv_out * post_norm_w).astype(jnp.bfloat16)
        return hidden_out, k_new, v_new

    cache_spec = P('dp', None, 'tp', None)
    return jax.shard_map(local_step, mesh=mesh, in_specs=(P('dp', None), P(None, 'tp'), P(None, 'tp'), P(None, 'tp'), P('tp', None), P('tp'), P('tp'), P(None), cache_spec, cache_spec, P('dp')), out_specs=(P('dp', None), cache_spec, cache_spec), check_vma=False)
```

profile of v0, /device:TPU:113, one launch (start us, length us, event | category | flops | bytes accessed | tf_op | source)
XLA Modules:
  0.0 264.2 jit_solution(7500678218227288350)
XLA Ops:
  7.2 0.0 copy-start
  7.2 0.1 all-reduce.2.cloned.1.call-start
  7.3 0.0 copy-start.2
  7.3 0.0 copy-start.6
  7.3 0.8 convert_element_type.69
  8.1 1.4 iota_compare_fusion.1
  9.5 3.8 %fusion.13 = (f32[1024]{0:T(1024)S(1)}, bf16[1024,256]{0,1:T(8,128)(2,1)S(1)}) fusion(bf16[1024,2048]{1,0:T(8,128)(2,1)} %param.11, bf16[2048,256]{1,0:T(8,128)(2,1)} %param.12), kind=kOutput, calls=%fused_computation.26 | convolution fusion | flops 1074789376 | bytes 5771264 | tf_op jit(solution)/shard_map/dot_general | solution.py:42
  13.3 0.0 copy-done.2
  13.3 0.0 copy-done.6
  13.3 0.0 copy-start.4
  13.4 0.0 copy-start.5
  13.4 1.3 fusion.16
  14.7 13.8 %psum.14 = f32[2,1024]{1,0:T(2,128)S(1)} all-reduce(f32[2,1024]{1,0:T(2,128)S(1)} %pad_maximum_fusion.1), channel_id=1, replica_groups=mesh['dp'=2,'tp'=8] {'tp'}, use_global_device_ids=true, to_apply=%region_2.0 | all-reduce | flops 2048 | bytes 16384 | tf_op jit(solution)/shard_map/psum | solution.py:46
  28.5 0.0 copy-done.4
  28.5 0.2 fusion.15
  28.7 0.1 convert.20
  28.8 0.0 copy-done.5
  28.8 0.2 fusion.18
  29.0 0.1 convert.21
  29.1 1.0 multiply_cosine_fusion
  30.1 0.4 subtract_convert_fusion
  30.5 0.9 maximum_convert_fusion
  31.5 0.6 copy.29
  32.0 1.3 copy.17
  33.4 84.4 %multiply_reduce_fusion = (f32[1024,2,32]{1,2,0:T(8,128)}, bf16[1024,32,2,128]{3,2,1,0:T(2,128)(2,1)}) fusion(f32[1024,2,128]{2,1,0:T(2,128)S(1)} %copy.29, bf16[1024,32,2,128]{3,2,1,0:T(2,128)(2,1)} %param.19, bf16[1024,2,128]{2,1,0:T(2,128)(2,1)S(1)} %copy.17, pred[1024,32]{1,0:T(8,128)(4,1)S(1)} %get-tuple-element.16), kind=kLoop, calls=%fused_computation.2 | loop fusion | flops 33488896 | bytes 35422208
  117.8 10.0 %copy.25 = f32[1024,2,32]{0,2,1:T(8,128)S(1)} copy(f32[1024,2,32]{1,2,0:T(8,128)} %get-tuple-element.3) | data formatting | bytes 524288 | tf_op jit(solution)/shard_map/bhd,bshd->bhs/dot_general | solution.py:31
  127.8 0.2 copy.16
  128.0 0.1 fusion.12
  128.1 0.7 copy.26
  128.9 3.8 %convolution_convert_fusion.1 = bf16[1024,256]{0,1:T(8,128)(2,1)S(1)} fusion(bf16[1024,2048]{1,0:T(8,128)(2,1)} %param.11, bf16[2048,256]{1,0:T(8,128)(2,1)} %param.14), kind=kOutput, calls=%fused_computation.18 | convolution fusion | flops 1074003968 | bytes 5767168 | tf_op jit(solution)/shard_map/dot_general | solution.py:44
  132.6 0.4 copy.18
  133.1 41.0 %broadcast_select_fusion = bf16[1024,32,2,128]{3,2,1,0:T(2,128)(2,1)S(1)} fusion(bf16[1024,32,2,128]{3,2,1,0:T(2,128)(2,1)} %param.20, pred[1024,32]{1,0:T(8,128)(4,1)S(1)} %get-tuple-element.16, bf16[1024,2,128]{2,1,0:T(2,128)(2,1)S(1)} %copy.18), kind=kLoop, calls=%fused_computation.3 | loop fusion | flops 8388608 | bytes 34111488 | tf_op jit(solution)/shard_map/jit(_where)/select_n | solution.py:26
  174.1 0.0 copy-start.1
  174.1 4.7 %fusion.2 = f32[1024,2,1,128]{3,2,1,0:T(1,128)S(1)} fusion(bf16[1024,2,32,1]{2,3,1,0:T(2,128)(2,1)S(1)} %copy.26, bf16[1024,32,2,128]{3,2,1,0:T(2,128)(2,1)S(1)} %broadcast_select_fusion), kind=kOutput, calls=%fused_computation.5 | convolution fusion | flops 16777216 | bytes 17956864 | tf_op jit(solution)/shard_map/bhs,bshd->bhd/dot_general | solution.py:35
  178.8 1.5 copy-done.1
  180.3 0.4 convert_element_type.75
  180.6 0.0 copy-start.3
  180.6 0.0 copy-done
  180.7 3.3 %convolution_convert_fusion = bf16[1024,2048]{1,0:T(8,128)(2,1)} fusion(bf16[256,2048]{1,0:T(8,128)(2,1)S(1)} %copy-done, bf16[128,8,2,128]{3,2,1,0:T(2,128)(2,1)S(1)} %bitcast.27), kind=kOutput, calls=%fused_computation.13 | convolution fusion | flops 1075838976 | bytes 5767168 | tf_op jit(solution)/shard_map/dot_general | solution.py:55
  183.9 0.1 all-reduce.2.cloned.1.call-update
  184.0 64.2 %all-reduce.2.cloned.1.call-done = bf16[1024,2048]{1,0:T(8,128)(2,1)} async-done(((bf16[1024,2048]{1,0:T(8,128)(2,1)}), bf16[1024,2048]{1,0:T(8,128)(2,1)}) %all-reduce.2.cloned.1.call-update) | async-done | bytes 4194320 | tf_op jit(solution)/shard_map/psum | solution.py:56
  248.2 3.1 %fusion.4 = f32[1024]{0:T(1024)S(1)} fusion(bf16[1024,2048]{1,0:T(8,128)(2,1)} %all-reduce.2.cloned.1.call-done), kind=kLoop, calls=%fused_computation.9 | loop fusion | flops 6290432 | bytes 4198400 | tf_op jit(solution)/shard_map/reduce_sum | solution.py:57
  251.2 0.0 copy-done.3
  251.2 6.1 %fusion.7 = bf16[1024,2048]{1,0:T(8,128)(2,1)} fusion(bf16[1024,2048]{1,0:T(8,128)(2,1)} %all-reduce.2.cloned.1.call-done, bf16[1024,2048]{1,0:T(8,128)(2,1)} %param.11, f32[2048]{0:T(1024)S(1)} %copy-done.3, f32[1024]{0:T(1024)S(1)} %add_rsqrt_fusion.1), kind=kLoop, calls=%fused_computation.12 | loop fusion | flops 12582912 | bytes 12595200 | tf_op jit(solution)/shard_map/convert_element_type | solution.py:58
  (5 shorter events, 0.1 us)
Async XLA Ops:
  7.2 173.5 %copy-start = (bf16[256,2048]{1,0:T(8,128)(2,1)S(1)}, bf16[256,2048]{1,0:T(8,128)(2,1)}, u32[]{:S(2)}) copy-start(bf16[256,2048]{1,0:T(8,128)(2,1)} %param.15) | copy-start | bytes 3145732
  7.2 241.0 %all-reduce.2.cloned.1.call-start = ((), (), s32[]{:S(2)}) async-start(), calls=%async_computation | async-start | bytes 8388608 | tf_op jit(solution)/shard_map/psum | solution.py:56
  7.3 6.1 %copy-start.2 = (bf16[1024,2048]{1,0:T(8,128)(2,1)S(1)}, bf16[1024,2048]{1,0:T(8,128)(2,1)}, u32[]{:S(2)}) copy-start(bf16[1024,2048]{1,0:T(8,128)(2,1)} %param.11) | copy-start | bytes 12582916
  7.3 6.1 %copy-start.6 = (bf16[2048,256]{1,0:T(8,128)(2,1)S(1)}, bf16[2048,256]{1,0:T(8,128)(2,1)}, u32[]{:S(2)}) copy-start(bf16[2048,256]{1,0:T(8,128)(2,1)} %param.13) | copy-start | bytes 3145732
  13.3 15.2 %copy-start.4 = (f32[256]{0:T(256)S(1)}, f32[256]{0:T(256)}, u32[]{:S(2)}) copy-start(f32[256]{0:T(256)} %param.16) | copy-start | bytes 3076
  13.4 15.5 %copy-start.5 = (f32[256]{0:T(256)S(1)}, f32[256]{0:T(256)}, u32[]{:S(2)}) copy-start(f32[256]{0:T(256)} %param.17) | copy-start | bytes 3076
  174.1 6.2 %copy-start.1 = (bf16[1024,32,2,128]{3,2,1,0:T(2,128)(2,1)}, bf16[1024,32,2,128]{3,2,1,0:T(2,128)(2,1)S(1)}, u32[]{:S(2)}) copy-start(bf16[1024,32,2,128]{3,2,1,0:T(2,128)(2,1)S(1)} %broadcast_select_fusion) | copy-start | bytes 50331652
  180.6 70.6 %copy-start.3 = (f32[2048]{0:T(1024)S(1)}, f32[2048]{0:T(1024)}, u32[]{:S(2)}) copy-start(f32[2048]{0:T(1024)} %param.18) | copy-start | bytes 24580
Sparse Core Ops, SparseCore 0:
  184.1 63.9 all-reduce.1
where the time goes:
time: 266 us; the launch traced here: 264 us
  other arithmetic  140 us (53%)
  waiting for transfers between devices  64.2 us (24%)
  matrix products  16.8 us (6%)
  local copies, waits for them, and re-layouts  14.7 us (6%)
  between operations  14.3 us (5%)
  blocking collectives  13.8 us (5%)
    unnamed x2, other arithmetic  85.3 us
    psum x1, waiting for transfers between devices, local_step(): a_out = lax.psum(proj_part, 'tp').astype(jnp.float32)  64.2 us
    select_n x1, other arithmetic, write_slot(): return jnp.where(at_slot, new_vals[:, None], cache)  41 us
    psum x1, blocking collectives, local_step(): energy = lax.psum(energy, 'tp')  13.8 us
    dot_general x1, local copies, waits for them, and re-layouts, attend(): jnp.einsum('bhd,bshd->bhs', q_rot, k_new, preferred_element_type=jnp.floa...  10 us
    convert_element_type x1, other arithmetic, local_step(): (hidden.astype(jnp.float32) + a_out * inv_out * post_norm_w).astype(jnp.b...  6.09 us
  transfers between devices with their start and end apart: 1, of which 1 were waited for; matrix products, arithmetic and copies ran while one was open for 0% of the time, Pallas kernels for 0%

commit v1 on v0

v1 whole, which is shorter than its diff:
```python
import functools
import math

import jax
import jax.numpy as jnp
import numpy as np
from jax import lax
from jax.experimental import pallas as pl
from jax.experimental.pallas import tpu as pltpu
from jax.sharding import PartitionSpec as P

NEG = -1e30

def attn_kernel(blk, nbuf, ahead, pos_s, pos_v, q_ref, kn_ref, vn_ref, kc_hbm, vc_hbm,
                o_ref, ko_hbm, vo_hbm, kbuf, vbuf, pcol, isem, osem):
    rows = q_ref.shape[0] * 8
    slots, heads, hd = kc_hbm.shape[1:]
    n_blk = rows // blk
    per_row = slots * heads
    scale2 = (hd ** -0.5) * math.log2(math.e)

    def cin(i, s):
        sl = pl.ds(i * blk, blk)
        return (pltpu.make_async_copy(kc_hbm.at[sl], kbuf.at[s], isem.at[0, s]),
                pltpu.make_async_copy(vc_hbm.at[sl], vbuf.at[s], isem.at[1, s]))

    def cout(i, s):
        sl = pl.ds(i * blk, blk)
        return (pltpu.make_async_copy(kbuf.at[s], ko_hbm.at[sl], osem.at[0, s]),
                pltpu.make_async_copy(vbuf.at[s], vo_hbm.at[sl], osem.at[1, s]))

    for j in range(ahead):
        for c in cin(j, j):
            c.start()

    lane = lax.broadcasted_iota(jnp.int32, (128, 128), 1)
    sub = lax.broadcasted_iota(jnp.int32, (128, 128), 0)
    for b in range(rows // 128):
        row = jnp.broadcast_to(pos_v[b:b + 1, :], (128, 128))
        col = jnp.sum(jnp.where(lane == sub, row, 0).astype(jnp.float32), axis=1, keepdims=True)
        pcol[pl.ds(b * 128, 128), :] = jnp.broadcast_to(col.astype(jnp.int32), (128, 128))

    ci = lax.broadcasted_iota(jnp.int32, (16, 8 * per_row), 1)
    ri = lax.broadcasted_iota(jnp.int32, (16, 8 * per_row), 0)
    match = jnp.logical_and(ci // per_row == ri % 8, ci % 2 == ri // 8)
    slotm = jnp.where(match, (ci % per_row) // 2, 1000)

    def body(i, carry):
        s = lax.rem(i, nbuf)
        nxt = i + ahead

        @pl.when(nxt < n_blk)
        def _():
            sn = lax.rem(nxt, nbuf)

            @pl.when(nxt >= nbuf)
            def _():
                for c in cout(0, sn):
                    c.wait()
            for c in cin(nxt, sn):
                c.start()
        for c in cin(0, s):
            c.wait()
        base = i * blk
        for r in range(blk):
            p = pos_s[base + r]
            kbuf[s, r, p] = kn_ref[base + r]
            vbuf[s, r, p] = vn_ref[base + r]
        kf = kbuf.at[s].reshape(blk * per_row, hd)
        vf = vbuf.at[s].reshape(blk * per_row, hd)
        for pair in range(blk // 16):
            ps = []
            for g in (2 * pair, 2 * pair + 1):
                qg = q_ref[i * (blk // 8) + g]
                kg = kf[pl.ds(g * 8 * per_row, 8 * per_row), :]
                sc = lax.dot_general(qg, kg, (((1,), (1,)), ((), ())), preferred_element_type=jnp.float32)
                pc = pcol[pl.ds(pl.multiple_of(base + g * 8, 8), 8), :]
                pc = jnp.concatenate([pc, pc], axis=0)
                pc = jnp.concatenate([pc] * (8 * per_row // 128), axis=1)
                sc = jnp.where(slotm <= pc, sc, NEG)
                m = jnp.max(sc, axis=1, keepdims=True)
                e = jnp.exp2((sc - m) * scale2)
                l = jnp.sum(e, axis=1, keepdims=True)
                ps.append((e / l).astype(jnp.bfloat16))
            pp = jnp.concatenate(ps, axis=0)
            va = vf[pl.ds(2 * pair * 8 * per_row, 8 * per_row), :]
            vb = vf[pl.ds((2 * pair + 1) * 8 * per_row, 8 * per_row), :]
            vv = jnp.concatenate([va, vb], axis=1)
            oo = jnp.dot(pp, vv, preferred_element_type=jnp.float32)
            h0 = jnp.concatenate([oo[0:8, :hd], oo[16:24, hd:]], axis=0)
            h1 = jnp.concatenate([oo[8:16, :hd], oo[24:32, hd:]], axis=0)
            rs = pl.ds(pl.multiple_of(base + pair * 16, 16), 16)
            o_ref[rs, 0:hd] = h0.astype(jnp.bfloat16)
            o_ref[rs, hd:2 * hd] = h1.astype(jnp.bfloat16)
        for c in cout(i, s):
            c.start()
        return carry

    lax.fori_loop(0, n_blk, body, 0)
    for j in range(min(nbuf, n_blk)):
        for c in cout(0, (n_blk - 1 - j) % nbuf):
            c.wait()


def attention(positions, qg, kn, vn, k_cache, v_cache, blk=64, nbuf=4, ahead=2):
    rows, slots, heads, hd = k_cache.shape
    vm = pl.BlockSpec(memory_space=pltpu.VMEM)
    anyspec = pl.BlockSpec(memory_space=pl.ANY)
    return pl.pallas_call(
        functools.partial(attn_kernel, blk, nbuf, ahead),
        out_shape=(jax.ShapeDtypeStruct((rows, heads * hd), jnp.bfloat16),
                   jax.ShapeDtypeStruct(k_cache.shape, k_cache.dtype),
                   jax.ShapeDtypeStruct(v_cache.shape, v_cache.dtype)),
        in_specs=[pl.BlockSpec(memory_space=pltpu.SMEM), vm, vm, vm, vm, anyspec, anyspec],
        out_specs=(vm, anyspec, anyspec),
        scratch_shapes=[
            pltpu.VMEM((nbuf, blk, slots, heads, hd), jnp.bfloat16),
            pltpu.VMEM((nbuf, blk, slots, heads, hd), jnp.bfloat16),
            pltpu.VMEM((rows, 128), jnp.int32),
            pltpu.SemaphoreType.DMA((2, nbuf)),
            pltpu.SemaphoreType.DMA((2, nbuf)),
        ],
        name='attn',
    )(positions, positions.reshape(rows // 128, 128), qg, kn, vn, k_cache, v_cache)


NORM_EPS = 1e-6
ROPE_BASE = 500000.0
MESH = pl.DeviceIdType.MESH
VMEM_SPEC = pl.BlockSpec(memory_space=pltpu.VMEM)
ANY_SPEC = pl.BlockSpec(memory_space=pl.ANY)
LANES = 128


def rope_table(slots, head_dim):
    half = head_dim // 2
    inv_freq = np.float32(ROPE_BASE) ** (np.float32(-2.0) * np.arange(half, dtype=np.float32) / np.float32(head_dim))
    angles = (np.arange(slots, dtype=np.float32)[:, None] * inv_freq[None, :].astype(np.float32)).astype(np.float64)
    cos, sin = np.cos(angles).astype(np.float32), np.sin(angles).astype(np.float32)
    full = np.concatenate([cos, cos, -sin, sin], axis=1)
    parts, rest = [], full
    for _ in range(3):
        part = rest.astype(jnp.bfloat16)
        parts.append(part)
        rest = rest - part.astype(np.float32)
    pad = np.zeros((LANES - 3 * slots, full.shape[1]), jnp.bfloat16)
    return np.concatenate(parts + [pad], axis=0)


def qkv_kernel(n, chunk, slots, pos_ref, tab_ref, qw_ref, kw_ref, hid_hbm, wq_hbm, wk_hbm, wv_hbm, wo_hbm,
               qg_ref, kn_ref, vn_ref, wop_hbm,
               hid, wq, wk, wv, qf, kf, stage, esend, erecv, lsem, osem, ssem, rsem):
    me = lax.axis_index('tp')
    rows, width = hid_hbm.shape
    cols = wq_hbm.shape[1]
    hd = qg_ref.shape[2]
    n_chunk = rows // chunk
    per = chunk // LANES

    loads = [pltpu.make_async_copy(wq_hbm, wq, lsem.at[0])]
    loads.append(pltpu.make_async_copy(hid_hbm.at[pl.ds(0, chunk)], hid.at[pl.ds(0, chunk)], lsem.at[3]))
    loads.append(pltpu.make_async_copy(wk_hbm, wk, lsem.at[1]))
    for c in range(1, n_chunk):
        loads.append(pltpu.make_async_copy(hid_hbm.at[pl.ds(c * chunk, chunk)], hid.at[pl.ds(c * chunk, chunk)], lsem.at[3 + c]))
    loads.append(pltpu.make_async_copy(wv_hbm, wv, lsem.at[2]))
    for cp in loads:
        cp.start()

    barrier = pltpu.get_barrier_semaphore()
    for d in range(1, n):
        pl.semaphore_signal(barrier, inc=1, device_id={'tp': lax.rem(me + d, n)}, device_id_type=MESH)

    lane = lax.broadcasted_iota(jnp.int32, (LANES, LANES), 1)
    sub = lax.broadcasted_iota(jnp.int32, (LANES, LANES), 0)
    eye = lane == sub

    def to_row(col):
        return jnp.sum(jnp.where(eye, jnp.broadcast_to(col, (LANES, LANES)), 0.0), axis=0, keepdims=True)

    def to_col(row):
        return jnp.sum(jnp.where(eye, jnp.broadcast_to(row, (LANES, LANES)), 0.0), axis=1, keepdims=True)

    def energy_copy(c, d):
        return pltpu.make_async_remote_copy(
            src_ref=esend.at[c], dst_ref=erecv.at[c, d - 1], send_sem=ssem.at[c, d - 1], recv_sem=rsem.at[c, d - 1],
            device_id={'tp': lax.rem(me + d, n)}, device_id_type=MESH)

    wo_copy = pltpu.make_async_remote_copy(
        src_ref=wo_hbm, dst_ref=wop_hbm, send_sem=osem.at[0], recv_sem=osem.at[1],
        device_id={'tp': me + 1 - 2 * lax.rem(me, 2)}, device_id_type=MESH)

    loads[0].wait()
    for c in range(n_chunk):
        loads[1 if c == 0 else 2 + c].wait()
        cs = pl.ds(c * chunk, chunk)
        rows_out = []
        for w, f, first in ((wq, qf, 0), (wk, kf, 1)):
            if c == 0 and first == 1:
                loads[2].wait()
            val = jnp.dot(hid[cs, :], w[...], preferred_element_type=jnp.float32).astype(jnp.bfloat16).astype(jnp.float32)
            f[cs, :] = val
            en = jnp.sum(val * val, axis=1, keepdims=True)
            for b in range(per):
                rows_out.append(to_row(en[b * LANES:(b + 1) * LANES]))
        pad = 8 - len(rows_out)
        esend[c] = jnp.concatenate(rows_out + [jnp.zeros((pad, LANES), jnp.float32)], axis=0)
        if c == 0:
            pl.semaphore_wait(barrier, n - 1)
            wo_copy.start()
        for d in range(1, n):
            energy_copy(c, d).start()

    loads[-1].wait()
    for c in range(n_chunk):
        cs = pl.ds(c * chunk, chunk)
        val = jnp.dot(hid[cs, :], wv[...], preferred_element_type=jnp.float32)
        stage[pl.ds(0, chunk, stride=2), :] = val[:, :hd]
        stage[pl.ds(1, chunk, stride=2), :] = val[:, hd:]
        vn_ref[pl.ds(c * 2 * chunk, 2 * chunk), :] = stage[...].astype(jnp.bfloat16)

    for c in range(n_chunk):
        total = esend[c]
        for d in range(1, n):
            energy_copy(c, d).wait_recv()
            total = total + erecv[c, d - 1]
        inv = lax.rsqrt(total / width + NORM_EPS)
        for b in range(per):
            base = c * chunk + b * LANES
            rs = pl.ds(base, LANES)
            p = to_col(pos_ref[c * per + b:c * per + b + 1, :].astype(jnp.float32)).astype(jnp.int32)
            hot = jnp.logical_and(lane < 3 * slots, lane % slots == p)
            trig = jnp.dot(jnp.where(hot, 1.0, 0.0).astype(jnp.bfloat16), tab_ref[...], preferred_element_type=jnp.float32)
            cos, sin = trig[:, :hd], trig[:, hd:]
            for f, w_ref, which in ((qf, qw_ref, 0), (kf, kw_ref, 1)):
                scale = to_col(inv[which * per + b:which * per + b + 1, :])
                normed = (f[rs, :] * scale * w_ref[...]).astype(jnp.bfloat16).astype(jnp.float32)
                rot = []
                for h in range(cols // hd):
                    x = normed[:, h * hd:(h + 1) * hd]
                    rot.append(x * cos + pltpu.roll(x, hd // 2, 1) * sin)
                if which == 0:
                    grouped = jnp.concatenate([r.reshape(LANES // 8, 8, hd) for r in rot], axis=1)
                    qg_ref[pl.ds(base // 8, LANES // 8)] = grouped.astype(jnp.bfloat16)
                else:
                    stage[pl.ds(0, LANES, stride=2), :] = rot[0]
                    stage[pl.ds(1, LANES, stride=2), :] = rot[1]
                    kn_ref[pl.ds(2 * base, 2 * LANES), :] = stage[pl.ds(0, 2 * LANES), :].astype(jnp.bfloat16)

    for c in range(n_chunk):
        for d in range(1, n):
            energy_copy(c, d).wait_send()
    wo_copy.wait()


def qkv(n, slots, heads, hd, positions, hidden, w_q, w_k, w_v, w_o, q_norm_w, k_norm_w, chunk=256):
    rows, width = hidden.shape
    cols = heads * hd
    n_chunk = rows // chunk
    f32, bf16 = jnp.float32, jnp.bfloat16
    return pl.pallas_call(
        functools.partial(qkv_kernel, n, chunk, slots),
        out_shape=(jax.ShapeDtypeStruct((rows // 8, 16, hd), bf16), jax.ShapeDtypeStruct((2 * rows, hd), bf16),
                   jax.ShapeDtypeStruct((2 * rows, hd), bf16), jax.ShapeDtypeStruct(w_o.shape, bf16)),
        in_specs=[VMEM_SPEC] * 4 + [ANY_SPEC] * 5,
        out_specs=(VMEM_SPEC, VMEM_SPEC, VMEM_SPEC, ANY_SPEC),
        scratch_shapes=[
            pltpu.VMEM((rows, width), bf16), pltpu.VMEM((width, cols), bf16), pltpu.VMEM((width, cols), bf16),
            pltpu.VMEM((width, cols), bf16), pltpu.VMEM((rows, cols), f32), pltpu.VMEM((rows, cols), f32),
            pltpu.VMEM((2 * chunk, hd), f32), pltpu.VMEM((n_chunk, 8, LANES), f32),
            pltpu.VMEM((n_chunk, n - 1, 8, LANES), f32),
            pltpu.SemaphoreType.DMA((3 + n_chunk,)), pltpu.SemaphoreType.DMA((2,)),
            pltpu.SemaphoreType.DMA((n_chunk, n - 1)), pltpu.SemaphoreType.DMA((n_chunk, n - 1)),
        ],
        compiler_params=pltpu.CompilerParams(collective_id=0, has_side_effects=True),
        name='qkv',
    )(positions.reshape(rows // LANES, LANES), jnp.asarray(rope_table(slots, hd)), q_norm_w.reshape(1, cols),
      k_norm_w.reshape(1, cols), hidden, w_q, w_k, w_v, w_o)


O, A_R, A_L, B_R, B_L, C_R, C_L, G1_R, G1_L, G2_R, G2_L, D_OWN, D_LEFT, D_RIGHT, D_ANT0, D_ANT1 = range(16)


def out_kernel(n, nj, o_ref, pw_ref, hid_hbm, wo_hbm, wop_hbm, out_ref,
               wo, wop, opart, part, hid, ra, rb, rc, cst, lsem, ssem, rsem):
    me = lax.axis_index('tp')
    nchip = n // 2
    chip, core = me // 2, lax.rem(me, 2)
    rows, width = out_ref.shape
    rc_rows = rows // nj
    half_rows = rc_rows // 2
    own = half_rows // nchip
    hf = own // 2
    xr, xl, xa = lax.rem(chip + 1, nchip), lax.rem(chip + nchip - 1, nchip), lax.rem(chip + 2, nchip)
    right, left, mate = xr * 2 + core, xl * 2 + core, chip * 2 + (1 - core)

    def qs(y, part_no, count):
        return pl.ds(pl.multiple_of(y * own + part_no * hf, hf), count)

    def gs(j, c, y, part_no, count):
        return pl.ds(pl.multiple_of(j * rc_rows + c * half_rows + y * own + part_no * hf, hf), count)

    def remote(kind, j, src, dst, dev):
        return pltpu.make_async_remote_copy(src_ref=src, dst_ref=dst, send_sem=ssem.at[kind, j], recv_sem=rsem.at[kind, j],
                                            device_id={'tp': dev}, device_id_type=MESH)

    sent = []

    def send(kind, j, src, dst, dev):
        cp = remote(kind, j, src, dst, dev)
        cp.start()
        sent.append(cp)

    def recv(kind, j, dst, dev):
        remote(kind, j, dst, dst, dev).wait_recv()

    lw = [pltpu.make_async_copy(wo_hbm, wo, lsem.at[0]), pltpu.make_async_copy(wop_hbm, wop, lsem.at[1])]
    lh = [pltpu.make_async_copy(hid_hbm.at[gs(j, core, chip, 0, own)], hid.at[j], lsem.at[2 + j]) for j in range(nj)]
    for cp in lw + lh:
        cp.start()

    barrier = pltpu.get_barrier_semaphore()
    for dev in (right, left, mate):
        pl.semaphore_signal(barrier, inc=1, device_id={'tp': dev}, device_id_type=MESH)
    pl.semaphore_wait(barrier, 3)

    for j in range(nj):
        src = pl.ds(pl.multiple_of(j * rc_rows + (1 - core) * half_rows, half_rows), half_rows)
        send(O, j, o_ref.at[src], opart.at[j], mate)

    def p1(j):
        if j == 0:
            lw[0].wait()
            lw[1].wait()
        recv(O, j, opart.at[j], mate)
        mine = o_ref[pl.ds(pl.multiple_of(j * rc_rows + core * half_rows, half_rows), half_rows), :]
        theirs = opart[j]
        step = 512
        for c0 in range(0, width, step):
            acc = jnp.dot(mine, wo[:, c0:c0 + step], preferred_element_type=jnp.float32)
            acc = acc + jnp.dot(theirs, wop[:, c0:c0 + step], preferred_element_type=jnp.float32)
            part[j, :, c0:c0 + step] = acc.astype(jnp.bfloat16)
        send(A_R, j, part.at[j, qs(xa, 0, hf)], ra.at[j, 0], right)
        send(A_L, j, part.at[j, qs(xa, 1, hf)], ra.at[j, 1], left)
        send(B_R, j, part.at[j, qs(xr, 1, hf)], rb.at[j, 0], right)
        send(B_L, j, part.at[j, qs(xl, 0, hf)], rb.at[j, 1], left)

    def p2(j):
        recv(A_R, j, ra.at[j, 0], left)
        cst[j, 0] = (part[j, qs(xr, 0, hf), :].astype(jnp.float32) + ra[j, 0].astype(jnp.float32)).astype(jnp.bfloat16)
        send(C_R, j, cst.at[j, 0], rc.at[j, 0], right)
        recv(A_L, j, ra.at[j, 1], right)
        cst[j, 1] = (part[j, qs(xl, 1, hf), :].astype(jnp.float32) + ra[j, 1].astype(jnp.float32)).astype(jnp.bfloat16)
        send(C_L, j, cst.at[j, 1], rc.at[j, 1], left)

    def p3(j):
        lh[j].wait()
        for k in range(2):
            recv((C_R, C_L)[k], j, rc.at[j, k], (left, right)[k])
            recv((B_L, B_R)[k], j, rb.at[j, 1 - k], (right, left)[k])
            a = (part[j, qs(chip, k, hf), :].astype(jnp.float32) + rc[j, k].astype(jnp.float32)
                 + rb[j, 1 - k].astype(jnp.float32))
            inv = lax.rsqrt(jnp.sum(a * a, axis=1, keepdims=True) / width + NORM_EPS)
            x = hid[j, k * hf:(k + 1) * hf, :].astype(jnp.float32)
            out_ref[gs(j, core, chip, k, hf), :] = (x + a * inv * pw_ref[...]).astype(jnp.bfloat16)
        blk = out_ref.at[gs(j, core, chip, 0, own)]
        send(G1_R, j, blk, blk, right)
        send(G1_L, j, blk, blk, left)
        send(D_OWN, j, blk, blk, mate)

    def p4(j):
        bl = out_ref.at[gs(j, core, xl, 0, own)]
        br = out_ref.at[gs(j, core, xr, 0, own)]
        recv(G1_R, j, bl, left)
        fl = out_ref.at[gs(j, core, xl, 0, hf)]
        send(G2_R, j, fl, fl, right)
        send(D_LEFT, j, bl, bl, mate)
        recv(G1_L, j, br, right)
        fr = out_ref.at[gs(j, core, xr, 1, hf)]
        send(G2_L, j, fr, fr, left)
        send(D_RIGHT, j, br, br, mate)

    def p5(j):
        b0 = out_ref.at[gs(j, core, xa, 0, hf)]
        recv(G2_R, j, b0, left)
        send(D_ANT0, j, b0, b0, mate)
        b1 = out_ref.at[gs(j, core, xa, 1, hf)]
        recv(G2_L, j, b1, right)
        send(D_ANT1, j, b1, b1, mate)

    stages = (p1, p2, p3, p4, p5)
    for t in range(nj + len(stages) - 1):
        for s, fn in enumerate(stages):
            if 0 <= t - s < nj:
                fn(t - s)
    for j in range(nj):
        oc = 1 - core
        recv(D_OWN, j, out_ref.at[gs(j, oc, chip, 0, own)], mate)
        recv(D_LEFT, j, out_ref.at[gs(j, oc, xl, 0, own)], mate)
        recv(D_RIGHT, j, out_ref.at[gs(j, oc, xr, 0, own)], mate)
        recv(D_ANT0, j, out_ref.at[gs(j, oc, xa, 0, hf)], mate)
        recv(D_ANT1, j, out_ref.at[gs(j, oc, xa, 1, hf)], mate)
    for cp in sent:
        cp.wait_send()


def project(n, attn, post_norm_w, hidden, w_o, w_o_mate, nj=4):
    rows, width = hidden.shape
    cols = attn.shape[1]
    half = rows // nj // 2
    own = half // (n // 2)
    hf = own // 2
    bf16 = jnp.bfloat16
    return pl.pallas_call(
        functools.partial(out_kernel, n, nj),
        out_shape=jax.ShapeDtypeStruct((rows, width), bf16),
        in_specs=[VMEM_SPEC, VMEM_SPEC, ANY_SPEC, ANY_SPEC, ANY_SPEC],
        out_specs=VMEM_SPEC,
        scratch_shapes=[
            pltpu.VMEM((cols, width), bf16), pltpu.VMEM((cols, width), bf16), pltpu.VMEM((nj, half, cols), bf16),
            pltpu.VMEM((nj, half, width), bf16), pltpu.VMEM((nj, own, width), bf16),
            pltpu.VMEM((nj, 2, hf, width), bf16), pltpu.VMEM((nj, 2, hf, width), bf16),
            pltpu.VMEM((nj, 2, hf, width), bf16), pltpu.VMEM((nj, 2, hf, width), bf16),
            pltpu.SemaphoreType.DMA((2 + nj,)), pltpu.SemaphoreType.DMA((16, nj)), pltpu.SemaphoreType.DMA((16, nj)),
        ],
        compiler_params=pltpu.CompilerParams(collective_id=1, has_side_effects=True),
        name='project',
    )(attn, post_norm_w.reshape(1, width), hidden, w_o, w_o_mate)


def solution(mesh):
    n = mesh.shape['tp']

    def local_step(hidden, w_q, w_k, w_v, w_o, q_norm_w, k_norm_w, post_norm_w, k_cache, v_cache, positions):
        rows, slots, heads, hd = k_cache.shape
        qg, kn, vn, w_o_mate = qkv(n, slots, heads, hd, positions, hidden, w_q, w_k, w_v, w_o, q_norm_w, k_norm_w)
        attn, k_new, v_new = attention(positions, qg, kn.reshape(rows, heads, hd), vn.reshape(rows, heads, hd), k_cache, v_cache)
        hidden_out = project(n, attn, post_norm_w, hidden, w_o, w_o_mate)
        return hidden_out, k_new, v_new

    cache_spec = P('dp', None, 'tp', None)
    return jax.shard_map(local_step, mesh=mesh, in_specs=(P('dp', None), P(None, 'tp'), P(None, 'tp'), P(None, 'tp'), P('tp', None), P('tp'), P('tp'), P(None), cache_spec, cache_spec, P('dp')), out_specs=(P('dp', None), cache_spec, cache_spec), check_vma=False)
```

time: 266 us -> 96.6 us (0.36)
  other arithmetic: 140 us -> 0 us
  Pallas kernels: 0 us -> 91 us
  waiting for transfers between devices: 64.2 us -> 0 us
  matrix products: 16.8 us -> 0 us
  blocking collectives: 13.8 us -> 0 us
  between operations: 14.3 us -> 0.66 us
  local copies, waits for them, and re-layouts: 14.7 us -> 4.79 us
    pallas_call x0 -> x3, Pallas kernels: none -> 91 us  [the longest x1 45 us: project(): pl.pallas_call(functools.partial(out_kernel, n, nj), out_shape=jax.ShapeD...]
    unnamed x2 -> x0, other arithmetic: 85.3 us -> none
    psum x1 -> x0, waiting for transfers between devices: 64.2 us -> none  [local_step(): a_out = lax.psum(proj_part, 'tp').astype(jnp.float32)]
    select_n x1 -> x0, other arithmetic: 41 us -> none  [write_slot(): return jnp.where(at_slot, new_vals[:, None], cache)]
    dot_general x5 -> x0, matrix products: 16.8 us -> none  [the longest x1 4.69 us: attend(): jnp.einsum('bhs,bshd->bhd', probs, v_new, preferred_element_type=jnp.floa...]
    psum x1 -> x0, blocking collectives: 13.8 us -> none  [local_step(): energy = lax.psum(energy, 'tp')]
    dot_general x1 -> x0, local copies, waits for them, and re-layouts: 10 us -> none  [attend(): jnp.einsum('bhd,bshd->bhs', q_rot, k_new, preferred_element_type=jnp.floa...]
    convert_element_type x7 -> x0, other arithmetic: 7.87 us -> none  [the longest x1 6.09 us: local_step(): (hidden.astype(jnp.float32) + a_out * inv_out * post_norm_w).astype(jnp.b...]
  transfers between devices with their start and end apart: 1 -> 0, of which waited for: 1 -> 0; matrix products, arithmetic and copies ran while one was open for 0% -> 0% of each run, Pallas kernels for 0% -> 0%
where the time goes in v1:
time: 96.6 us; the launch traced here: 96.4 us
  Pallas kernels  91 us (94%)
  local copies, waits for them, and re-layouts  4.79 us (5%)
    pallas_call x1, Pallas kernels, project(): pl.pallas_call(functools.partial(out_kernel, n, nj), out_shape=jax.ShapeD...  45 us
    pallas_call x1, Pallas kernels, attention(): pl.pallas_call(functools.partial(attn_kernel, blk, nbuf, ahead), out_shap...  30.8 us
    pallas_call x1, Pallas kernels, qkv(): pl.pallas_call(functools.partial(qkv_kernel, n, chunk, slots), out_shape=...  15.2 us
    unnamed x1, local copies, waits for them, and re-layouts  4.79 us

profile of v1, /device:TPU:113, one launch (start us, length us, event | category | flops | bytes accessed | tf_op | source)
XLA Modules:
  0.0 96.4 jit_solution(16001584022884678311)
XLA Ops:
  0.6 15.2 %qkv.1 = (bf16[128,16,128]{2,1,0:T(8,128)(2,1)}, bf16[2048,128]{1,0:T(8,128)(2,1)}, bf16[2048,128]{1,0:T(8,128)(2,1)}, bf16[256,2048]{1,0:T(8,128)(2,1)}) custom-call(s32[8,128]{1,0:T(8,128)} %bitcast.8, bf16[128,256]{1,0:T(8,128)(2,1)} %constant.2.clone.tab_ref, f32[1,256]{1,0:T(1,128)} %bitcast.11, f32[1,256]{1,0:T(1,128)} %bitcast.12, ...), custom_call_target="tpu_custom_call" | custom-call | tf_op jit(solution)/shard_map/qkv/pallas_call | solution.py:260
  15.8 30.8 %attn.1 = (bf16[1024,256]{1,0:T(8,128)(2,1)}, bf16[1024,32,2,128]{3,2,1,0:T(2,128)(2,1)}, bf16[1024,32,2,128]{3,2,1,0:T(2,128)(2,1)}) custom-call(s32[1024]{0:T(1024)} %pos_s.1, s32[8,128]{1,0:T(8,128)} %bitcast.9, bf16[128,16,128]{2,1,0:T(8,128)(2,1)} %get-tuple-element.10.q_ref, bf16[1024,2,128]{2,1,0:T(2,128)(2,1)} %bitcast.6, ...), custom_call_target="tpu_custom_call" | custom-call | tf_op jit(solution)/shard_map/attn/pallas_call | solution.py:109
  46.6 45.0 %project.1 = bf16[1024,2048]{1,0:T(8,128)(2,1)} custom-call(bf16[1024,256]{1,0:T(8,128)(2,1)} %get-tuple-element.13.o_ref, f32[1,2048]{1,0:T(1,128)} %bitcast.10, bf16[1024,2048]{1,0:T(8,128)(2,1)} %hid_hbm.3, bf16[256,2048]{1,0:T(8,128)(2,1)} %wo_hbm.3, bf16[256,2048]{1,0:T(8,128)(2,1)} %get-tuple-element.14.wop_hbm), custom_call_target="tpu_custom_call" | custom-call | tf_op jit(solution)/shard_map/project/pallas_call | solution.py:413
  91.6 4.8 %copy.16 = bf16[1024,2048]{1,0:T(8,128)(2,1)} copy(bf16[1024,2048]{1,0:T(8,128)(2,1)} %project.1) | data formatting | bytes 8388608

commit v2 on v0

v2 whole, which is shorter than its diff:
```python
import functools
import math

import jax
import jax.numpy as jnp
import numpy as np
from jax import lax
from jax.experimental import pallas as pl
from jax.experimental.pallas import tpu as pltpu
from jax.sharding import PartitionSpec as P

NORM_EPS = 1e-6
ROPE_BASE = 500000.0
NEG = -1e30
MESH = pl.DeviceIdType.MESH
VMEM_SPEC = pl.BlockSpec(memory_space=pltpu.VMEM)
HBM_SPEC = pl.BlockSpec(memory_space=pltpu.HBM)
LANES = 128
BLK = 64


def rope_table(slots, head_dim):
    half = head_dim // 2
    inv_freq = np.float32(ROPE_BASE) ** (np.float32(-2.0) * np.arange(half, dtype=np.float32) / np.float32(head_dim))
    angles = (np.arange(slots, dtype=np.float32)[:, None] * inv_freq[None, :].astype(np.float32)).astype(np.float64)
    cos, sin = np.cos(angles).astype(np.float32), np.sin(angles).astype(np.float32)
    full = np.concatenate([cos, cos, -sin, sin], axis=1)
    parts, rest = [], full
    for _ in range(3):
        part = rest.astype(jnp.bfloat16)
        parts.append(part)
        rest = rest - part.astype(np.float32)
    pad = np.zeros((LANES - 3 * slots, full.shape[1]), jnp.bfloat16)
    return np.concatenate(parts + [pad], axis=0)


O, A_R, A_L, B_R, B_L, C_R, C_L, G1_R, G1_L, G2_R, G2_L, D_OWN, D_LEFT, D_RIGHT, D_ANT0, D_ANT1 = range(16)


def step_kernel(n, nj, slots, heads, hd,
                pos_ref, tab_ref, qw_ref, kw_ref, pw_ref, hid_hbm, wq_hbm, wk_hbm, wv_hbm, wo_hbm, kc_hbm, vc_hbm,
                kc, vc, out_ref, kn_hbm, vn_hbm,
                kn, vn, hid, wq, wk, wv, wo, wop, qf, kf, qg, pcol, s_scr, p_scr, o_scr, opart, part, ra, rb, rc, cst,
                esend, erecv, lsem, csem, nsem, osem, essem, ersem, ssem, rsem):
    me = lax.axis_index('tp')
    rows, width = hid_hbm.shape
    cols = heads * hd
    per_row = slots * heads
    rc_rows = rows // nj
    per = rc_rows // LANES
    nchip = n // 2
    chip, core = me // 2, lax.rem(me, 2)
    half_rows = rc_rows // 2
    own = half_rows // nchip
    hf = own // 2
    xr, xl, xa = lax.rem(chip + 1, nchip), lax.rem(chip + nchip - 1, nchip), lax.rem(chip + 2, nchip)
    right, left, mate = xr * 2 + core, xl * 2 + core, chip * 2 + (1 - core)
    f32, bf16 = jnp.float32, jnp.bfloat16

    def chunk(c):
        return pl.ds(c * rc_rows, rc_rows)

    ld_w = [pltpu.make_async_copy(src, dst, lsem.at[k]) for k, (src, dst) in
            enumerate(((wq_hbm, wq), (wk_hbm, wk), (wv_hbm, wv), (wo_hbm, wo)))]
    ld_h = [pltpu.make_async_copy(hid_hbm.at[chunk(c)], hid.at[chunk(c)], lsem.at[4 + c]) for c in range(nj)]

    def ld_kv(c):
        sl = pl.ds(c * rc_rows * per_row, rc_rows * per_row)
        return [pltpu.make_async_copy(kc_hbm.at[sl], kc.at[sl], csem.at[0, c]),
                pltpu.make_async_copy(vc_hbm.at[sl], vc.at[sl], csem.at[1, c])]

    for cp in (ld_h[0], ld_w[0], ld_w[1], ld_w[2], ld_h[1]):
        cp.start()

    barrier = pltpu.get_barrier_semaphore()
    for d in range(1, n):
        pl.semaphore_signal(barrier, inc=1, device_id={'tp': lax.rem(me + d, n)}, device_id_type=MESH)

    lane = lax.broadcasted_iota(jnp.int32, (LANES, LANES), 1)
    sub = lax.broadcasted_iota(jnp.int32, (LANES, LANES), 0)
    eye = lane == sub
    span = 8 * per_row
    ci = lax.broadcasted_iota(jnp.int32, (16, span), 1)
    ri = lax.broadcasted_iota(jnp.int32, (16, span), 0)
    match = jnp.logical_and(ci // per_row == ri % 8, ci % heads == ri // 8)
    slotm = jnp.where(match, (ci % per_row) // heads, 1000)
    scale2 = (hd ** -0.5) * math.log2(math.e)

    def to_row(col):
        return jnp.sum(jnp.where(eye, jnp.broadcast_to(col, (LANES, LANES)), 0.0), axis=0, keepdims=True)

    def to_col(row):
        return jnp.sum(jnp.where(eye, jnp.broadcast_to(row, (LANES, LANES)), 0.0), axis=1, keepdims=True)

    def energy_copy(c, d):
        return pltpu.make_async_remote_copy(
            src_ref=esend.at[c], dst_ref=erecv.at[c, d - 1], send_sem=essem.at[c, d - 1], recv_sem=ersem.at[c, d - 1],
            device_id={'tp': lax.rem(me + d, n)}, device_id_type=MESH)

    wo_copy = pltpu.make_async_remote_copy(
        src_ref=wo_hbm, dst_ref=wop, send_sem=osem.at[0], recv_sem=osem.at[1],
        device_id={'tp': mate}, device_id_type=MESH)

    def project_qkv(c):
        cs = chunk(c)
        ld_h[c].wait()
        rows_out = []
        for k, (w, f) in enumerate(((wq, qf), (wk, kf))):
            if c == 0:
                ld_w[k].wait()
            val = jnp.dot(hid[cs, :], w[...], preferred_element_type=f32).astype(bf16).astype(f32)
            f[cs, :] = val
            en = jnp.sum(val * val, axis=1, keepdims=True)
            for b in range(per):
                rows_out.append(to_row(en[b * LANES:(b + 1) * LANES]))
        pad = 8 - len(rows_out)
        esend[c] = jnp.concatenate(rows_out + [jnp.zeros((pad, LANES), f32)], axis=0)
        if c == 0:
            pl.semaphore_wait(barrier, n - 1)
        for d in range(1, n):
            energy_copy(c, d).start()
        if c == 0:
            ld_w[2].wait()
            for cp in ld_kv(0) + ld_h[2:] + [ld_w[3]]:
                cp.start()
            wo_copy.start()
        val = jnp.dot(hid[cs, :], wv[...], preferred_element_type=f32).astype(bf16).astype(f32)
        for h in range(heads):
            vn[h, cs, :] = val[:, h * hd:(h + 1) * hd]

    def norm_rope(c):
        total = esend[c]
        for d in range(1, n):
            energy_copy(c, d).wait_recv()
            total = total + erecv[c, d - 1]
        inv = lax.rsqrt(total / width + NORM_EPS)
        for b in range(per):
            base = c * rc_rows + b * LANES
            rs = pl.ds(base, LANES)
            p = to_col(pos_ref[c * per + b:c * per + b + 1, :].astype(f32)).astype(jnp.int32)
            pcol[rs, :] = jnp.broadcast_to(p, (LANES, LANES))
            hot = jnp.logical_and(lane < 3 * slots, lane % slots == p)
            trig = jnp.dot(jnp.where(hot, 1.0, 0.0).astype(bf16), tab_ref[...], preferred_element_type=f32)
            cos, sin = trig[:, :hd], trig[:, hd:]
            for f, w_ref, which in ((qf, qw_ref, 0), (kf, kw_ref, 1)):
                scale = to_col(inv[which * per + b:which * per + b + 1, :])
                normed = (f[rs, :] * scale * w_ref[...]).astype(bf16).astype(f32)
                rot = []
                for h in range(heads):
                    x = normed[:, h * hd:(h + 1) * hd]
                    rot.append(x * cos + pltpu.roll(x, hd // 2, 1) * sin)
                if which == 0:
                    grouped = jnp.concatenate([r.reshape(LANES // 8, 8, hd) for r in rot], axis=1)
                    qg[pl.ds(base // 8, LANES // 8)] = grouped.astype(bf16)
                else:
                    for h in range(heads):
                        kn[h, rs, :] = rot[h].astype(bf16).astype(f32)

    def attend_block(i, carry):
        base = i * BLK
        n_grp = BLK // 8

        def kv_rows(g, count):
            return pl.ds(pl.multiple_of(base * per_row + g * span, span), count * span)

        for g in range(n_grp):
            s_scr[pl.ds(g * 16, 16), :] = lax.dot_general(
                qg[i * n_grp + g], kc[kv_rows(g, 1), :], (((1,), (1,)), ((), ())), preferred_element_type=f32)
        p_new = []
        for g in range(n_grp):
            r8 = pl.ds(pl.multiple_of(base + g * 8, 8), 8)
            pc = jnp.concatenate([pcol[r8, :]] * heads, axis=0)
            wide_pc = jnp.concatenate([pc] * (span // LANES), axis=1)
            k_own = jnp.concatenate([kn[h, r8, :] for h in range(heads)], axis=0)
            s_own = jnp.sum(qg[i * n_grp + g].astype(f32) * k_own, axis=1, keepdims=True)
            sc = jnp.where(slotm < wide_pc, s_scr[pl.ds(g * 16, 16), :], NEG)
            top = jnp.maximum(jnp.max(sc, axis=1, keepdims=True), s_own)
            e = jnp.exp2((sc - top) * scale2)
            e_own = jnp.exp2((s_own - top) * scale2)
            inv_l = 1.0 / (jnp.sum(e, axis=1, keepdims=True) + e_own)
            p_scr[pl.ds(g * 16, 16), :] = (e * inv_l).astype(bf16)
            p_new.append((e_own * inv_l).astype(bf16).astype(f32))
        for pair in range(n_grp // 2):
            vv = jnp.concatenate([vc[kv_rows(2 * pair, 1), :], vc[kv_rows(2 * pair + 1, 1), :]], axis=1)
            oo = jnp.dot(p_scr[pl.ds(pair * 32, 32), :], vv, preferred_element_type=f32)
            res = []
            for t in range(2):
                g = 2 * pair + t
                r8 = pl.ds(pl.multiple_of(base + g * 8, 8), 8)
                v_own = jnp.concatenate([vn[h, r8, :] for h in range(heads)], axis=0)
                res.append(oo[16 * t:16 * t + 16, t * hd:(t + 1) * hd] + p_new[g] * v_own)
            rs = pl.ds(pl.multiple_of(base + pair * 16, 16), 16)
            for h in range(heads):
                o_scr[rs, h * hd:(h + 1) * hd] = jnp.concatenate(
                    [res[0][8 * h:8 * h + 8], res[1][8 * h:8 * h + 8]], axis=0).astype(bf16)
        return carry

    blocks = rc_rows // BLK

    def attend(c, first, count):
        if first == 0:
            for cp in ld_kv(c):
                cp.wait()
            if c + 1 < nj:
                for cp in ld_kv(c + 1):
                    cp.start()
        lax.fori_loop(c * blocks + first, c * blocks + first + count, attend_block, 0)

    def qs(y, part_no, count):
        return pl.ds(pl.multiple_of(y * own + part_no * hf, hf), count)

    def gs(j, c, y, part_no, count):
        return pl.ds(pl.multiple_of(j * rc_rows + c * half_rows + y * own + part_no * hf, hf), count)

    def remote(kind, j, src, dst, dev):
        return pltpu.make_async_remote_copy(src_ref=src, dst_ref=dst, send_sem=ssem.at[kind, j], recv_sem=rsem.at[kind, j],
                                            device_id={'tp': dev}, device_id_type=MESH)

    sent = []

    def send(kind, j, src, dst, dev):
        cp = remote(kind, j, src, dst, dev)
        cp.start()
        sent.append(cp)

    def recv(kind, j, dst, dev):
        remote(kind, j, dst, dst, dev).wait_recv()

    def p0(j):
        src = pl.ds(pl.multiple_of(j * rc_rows + (1 - core) * half_rows, half_rows), half_rows)
        send(O, j, o_scr.at[src], opart.at[j], mate)

    def p1(j):
        if j == 0:
            ld_w[3].wait()
            wo_copy.wait_recv()
        recv(O, j, opart.at[j], mate)
        mine = o_scr[pl.ds(pl.multiple_of(j * rc_rows + core * half_rows, half_rows), half_rows), :]
        theirs = opart[j]
        step = 512
        for c0 in range(0, width, step):
            acc = jnp.dot(mine, wo[:, c0:c0 + step], preferred_element_type=f32)
            acc = acc + jnp.dot(theirs, wop[:, c0:c0 + step], preferred_element_type=f32)
            part[j, :, c0:c0 + step] = acc.astype(bf16)
        send(A_R, j, part.at[j, qs(xa, 0, hf)], ra.at[j, 0], right)
        send(A_L, j, part.at[j, qs(xa, 1, hf)], ra.at[j, 1], left)
        send(B_R, j, part.at[j, qs(xr, 1, hf)], rb.at[j, 0], right)
        send(B_L, j, part.at[j, qs(xl, 0, hf)], rb.at[j, 1], left)

    def p2(j):
        recv(A_R, j, ra.at[j, 0], left)
        cst[j, 0] = (part[j, qs(xr, 0, hf), :].astype(f32) + ra[j, 0].astype(f32)).astype(bf16)
        send(C_R, j, cst.at[j, 0], rc.at[j, 0], right)
        recv(A_L, j, ra.at[j, 1], right)
        cst[j, 1] = (part[j, qs(xl, 1, hf), :].astype(f32) + ra[j, 1].astype(f32)).astype(bf16)
        send(C_L, j, cst.at[j, 1], rc.at[j, 1], left)

    def p3(j):
        for k in range(2):
            recv((C_R, C_L)[k], j, rc.at[j, k], (left, right)[k])
            recv((B_L, B_R)[k], j, rb.at[j, 1 - k], (right, left)[k])
            a = (part[j, qs(chip, k, hf), :].astype(f32) + rc[j, k].astype(f32) + rb[j, 1 - k].astype(f32))
            inv = lax.rsqrt(jnp.sum(a * a, axis=1, keepdims=True) / width + NORM_EPS)
            mine = gs(j, core, chip, k, hf)
            out_ref[mine, :] = (hid[mine, :].astype(f32) + a * inv * pw_ref[...]).astype(bf16)
        blk = out_ref.at[gs(j, core, chip, 0, own)]
        send(G1_R, j, blk, blk, right)
        send(G1_L, j, blk, blk, left)
        send(D_OWN, j, blk, blk, mate)

    def p4(j):
        bl = out_ref.at[gs(j, core, xl, 0, own)]
        br = out_ref.at[gs(j, core, xr, 0, own)]
        recv(G1_R, j, bl, left)
        fl = out_ref.at[gs(j, core, xl, 0, hf)]
        send(G2_R, j, fl, fl, right)
        send(D_LEFT, j, bl, bl, mate)
        recv(G1_L, j, br, right)
        fr = out_ref.at[gs(j, core, xr, 1, hf)]
        send(G2_L, j, fr, fr, left)
        send(D_RIGHT, j, br, br, mate)

    def p5(j):
        b0 = out_ref.at[gs(j, core, xa, 0, hf)]
        recv(G2_R, j, b0, left)
        send(D_ANT0, j, b0, b0, mate)
        b1 = out_ref.at[gs(j, core, xa, 1, hf)]
        recv(G2_L, j, b1, right)
        send(D_ANT1, j, b1, b1, mate)

    new_out = [pltpu.make_async_copy(kn, kn_hbm, nsem.at[0]), pltpu.make_async_copy(vn, vn_hbm, nsem.at[1])]
    qh, kh = blocks // 2, blocks - blocks // 2
    project_qkv(0)
    project_qkv(1)
    norm_rope(0)
    attend(0, 0, blocks)
    p0(0)
    norm_rope(1)
    p1(0)
    attend(1, 0, qh)
    p2(0)
    attend(1, qh, kh)
    p0(1)
    project_qkv(2)
    p1(1)
    p3(0)
    norm_rope(2)
    attend(2, 0, qh)
    p2(1)
    p4(0)
    attend(2, qh, kh)
    p0(2)
    project_qkv(3)
    p1(2)
    p3(1)
    p5(0)
    norm_rope(3)
    for cp in new_out:
        cp.start()
    attend(3, 0, qh)
    p2(2)
    p4(1)
    attend(3, qh, kh)
    p0(3)
    p1(3)
    p3(2)
    p5(1)
    p2(3)
    p4(2)
    p3(3)
    p5(2)
    p4(3)
    p5(3)
    for j in range(nj):
        oc = 1 - core
        recv(D_OWN, j, out_ref.at[gs(j, oc, chip, 0, own)], mate)
        recv(D_LEFT, j, out_ref.at[gs(j, oc, xl, 0, own)], mate)
        recv(D_RIGHT, j, out_ref.at[gs(j, oc, xr, 0, own)], mate)
        recv(D_ANT0, j, out_ref.at[gs(j, oc, xa, 0, hf)], mate)
        recv(D_ANT1, j, out_ref.at[gs(j, oc, xa, 1, hf)], mate)
    for cp in sent:
        cp.wait_send()
    for c in range(nj):
        for d in range(1, n):
            energy_copy(c, d).wait_send()
    wo_copy.wait_send()
    for cp in new_out:
        cp.wait()


def decode_step(n, slots, heads, hd, positions, hidden, w_q, w_k, w_v, w_o, q_norm_w, k_norm_w, post_norm_w, k_flat, v_flat, nj=4):
    rows, width = hidden.shape
    cols = heads * hd
    rc_rows = rows // nj
    half = rc_rows // 2
    own = half // (n // 2)
    hf = own // 2
    span = 8 * slots * heads
    f32, bf16 = jnp.float32, jnp.bfloat16
    dma = pltpu.SemaphoreType.DMA
    return pl.pallas_call(
        functools.partial(step_kernel, n, nj, slots, heads, hd),
        out_shape=(pltpu.VMEM(k_flat.shape, bf16), pltpu.VMEM(v_flat.shape, bf16), pltpu.VMEM((rows, width), bf16),
                   jax.ShapeDtypeStruct((heads, rows, hd), f32), jax.ShapeDtypeStruct((heads, rows, hd), f32)),
        in_specs=[VMEM_SPEC] * 5 + [HBM_SPEC] * 7,
        out_specs=(VMEM_SPEC,) * 3 + (HBM_SPEC,) * 2,
        scratch_shapes=[
            pltpu.VMEM((heads, rows, hd), f32), pltpu.VMEM((heads, rows, hd), f32),
            pltpu.VMEM((rows, width), bf16), pltpu.VMEM((width, cols), bf16), pltpu.VMEM((width, cols), bf16),
            pltpu.VMEM((width, cols), bf16), pltpu.VMEM((cols, width), bf16), pltpu.VMEM((cols, width), bf16),
            pltpu.VMEM((rows, cols), f32), pltpu.VMEM((rows, cols), f32), pltpu.VMEM((rows // 8, 8 * heads, hd), bf16),
            pltpu.VMEM((rows, LANES), jnp.int32), pltpu.VMEM((BLK * heads, span), f32), pltpu.VMEM((BLK * heads, span), bf16),
            pltpu.VMEM((rows, cols), bf16), pltpu.VMEM((nj, half, cols), bf16), pltpu.VMEM((nj, half, width), bf16),
            pltpu.VMEM((nj, 2, hf, width), bf16), pltpu.VMEM((nj, 2, hf, width), bf16),
            pltpu.VMEM((nj, 2, hf, width), bf16), pltpu.VMEM((nj, 2, hf, width), bf16),
            pltpu.VMEM((nj, 8, LANES), f32), pltpu.VMEM((nj, n - 1, 8, LANES), f32),
            dma((4 + nj,)), dma((2, nj)), dma((2,)), dma((2,)), dma((nj, n - 1)), dma((nj, n - 1)), dma((16, nj)), dma((16, nj)),
        ],
        compiler_params=pltpu.CompilerParams(collective_id=0, has_side_effects=True, vmem_limit_bytes=26 << 20),
        name='decode_step',
    )(positions.reshape(rows // LANES, LANES), jnp.asarray(rope_table(slots, hd)), q_norm_w.reshape(1, cols),
      k_norm_w.reshape(1, cols), post_norm_w.reshape(1, width), hidden, w_q, w_k, w_v, w_o, k_flat, v_flat)


def store_kernel(blk, slots, heads, hd, pos_s, kn, vn, kc, vc, ko, vo, kc_alias, vc_alias, mtab, sem):
    rows = kn.shape[1]
    per_row = slots * heads
    even = lax.broadcasted_iota(jnp.int32, (8, hd), 0) % heads == 0
    pair_id = lax.broadcasted_iota(jnp.int32, (8, hd), 0) // heads
    for k in range(4):
        mtab[k] = jnp.where(pair_id == k, 1.0, 0.0).astype(jnp.bfloat16)

    def copies(i):
        sl = pl.ds(pl.multiple_of(i * blk * per_row, blk * per_row), blk * per_row)
        return [pltpu.make_async_copy(kc_alias.at[sl], ko.at[sl], sem.at[0, i]),
                pltpu.make_async_copy(vc_alias.at[sl], vo.at[sl], sem.at[1, i])]

    def body(i, carry):
        base = i * blk
        for r in range(blk):
            p = pos_s[base + r]
            at = pl.ds(pl.multiple_of((base + r) * per_row + lax.shift_left(lax.shift_right_logical(p, 2), 3), 8), 8)
            hit = mtab[p & 3] > 0
            row = pl.ds(base + r, 8, stride=0)
            for src, dst in ((kn, kc_alias), (vn, vc_alias)):
                new = jnp.where(even, src[0, row, :], src[1, row, :]).astype(jnp.bfloat16)
                dst[at, :] = jnp.where(hit, new, dst[at, :])
        for cp in copies(i):
            cp.start()
        return carry

    lax.fori_loop(0, rows // blk, body, 0)
    for i in range(rows // blk):
        for cp in copies(i):
            cp.wait()


def store(positions, kn, vn, k_vm, v_vm, slots, heads, hd, blk=64):
    rows = kn.shape[1]
    bf16 = jnp.bfloat16
    dma = pltpu.SemaphoreType.DMA
    res = pl.pallas_call(
        functools.partial(store_kernel, blk, slots, heads, hd),
        out_shape=(jax.ShapeDtypeStruct(k_vm.shape, bf16),
                   jax.ShapeDtypeStruct(v_vm.shape, bf16), pltpu.VMEM(k_vm.shape, bf16), pltpu.VMEM(v_vm.shape, bf16)),
        in_specs=[pl.BlockSpec(memory_space=pltpu.SMEM)] + [VMEM_SPEC] * 4,
        out_specs=(HBM_SPEC, HBM_SPEC, VMEM_SPEC, VMEM_SPEC),
        input_output_aliases={3: 2, 4: 3},
        scratch_shapes=[pltpu.VMEM((4, 8, hd), bf16), dma((2, rows // blk))],
        compiler_params=pltpu.CompilerParams(vmem_limit_bytes=26 << 20),
        name='store',
    )(positions, kn, vn, k_vm, v_vm)
    return res[:2]


def solution(mesh):
    n = mesh.shape['tp']

    def local_step(hidden, w_q, w_k, w_v, w_o, q_norm_w, k_norm_w, post_norm_w, k_cache, v_cache, positions):
        rows, slots, heads, hd = k_cache.shape
        flat = (rows * slots * heads, hd)
        k_vm, v_vm, hid_vm, kn, vn = decode_step(n, slots, heads, hd, positions, hidden, w_q, w_k, w_v, w_o, q_norm_w,
                                                 k_norm_w, post_norm_w, k_cache.reshape(flat), v_cache.reshape(flat))
        k_new, v_new = store(positions, kn, vn, k_vm, v_vm, slots, heads, hd)
        return hid_vm, k_new.reshape(k_cache.shape), v_new.reshape(v_cache.shape)

    cache_spec = P('dp', None, 'tp', None)
    return jax.shard_map(local_step, mesh=mesh, in_specs=(P('dp', None), P(None, 'tp'), P(None, 'tp'), P(None, 'tp'), P('tp', None), P('tp'), P('tp'), P(None), cache_spec, cache_spec, P('dp')), out_specs=(P('dp', None), cache_spec, cache_spec), check_vma=False)
```

time: 266 us -> 82.8 us (0.31)
  other arithmetic: 140 us -> 0 us
  Pallas kernels: 0 us -> 79.8 us
  waiting for transfers between devices: 64.2 us -> 0 us
  matrix products: 16.8 us -> 0 us
  blocking collectives: 13.8 us -> 0 us
  between operations: 14.3 us -> 0.8 us
  local copies, waits for them, and re-layouts: 14.7 us -> 2.02 us
    unnamed x2 -> x0, other arithmetic: 85.3 us -> none
    pallas_call x0 -> x2, Pallas kernels: none -> 79.8 us  [the longest x1 66.8 us: decode_step(): pl.pallas_call(functools.partial(step_kernel, n, nj, slots, heads, hd), o...]
    psum x1 -> x0, waiting for transfers between devices: 64.2 us -> none  [local_step(): a_out = lax.psum(proj_part, 'tp').astype(jnp.float32)]
    select_n x1 -> x0, other arithmetic: 41 us -> none  [write_slot(): return jnp.where(at_slot, new_vals[:, None], cache)]
    dot_general x5 -> x0, matrix products: 16.8 us -> none  [the longest x1 4.69 us: attend(): jnp.einsum('bhs,bshd->bhd', probs, v_new, preferred_element_type=jnp.floa...]
    psum x1 -> x0, blocking collectives: 13.8 us -> none  [local_step(): energy = lax.psum(energy, 'tp')]
    dot_general x1 -> x0, local copies, waits for them, and re-layouts: 10 us -> none  [attend(): jnp.einsum('bhd,bshd->bhs', q_rot, k_new, preferred_element_type=jnp.floa...]
    convert_element_type x7 -> x0, other arithmetic: 7.87 us -> none  [the longest x1 6.09 us: local_step(): (hidden.astype(jnp.float32) + a_out * inv_out * post_norm_w).astype(jnp.b...]
  transfers between devices with their start and end apart: 1 -> 0, of which waited for: 1 -> 0; matrix products, arithmetic and copies ran while one was open for 0% -> 0% of each run, Pallas kernels for 0% -> 0%
where the time goes in v2:
time: 82.8 us; the launch traced here: 82.6 us
  Pallas kernels  79.8 us (96%)
  local copies, waits for them, and re-layouts  2.02 us (2%)
    pallas_call x1, Pallas kernels, decode_step(): pl.pallas_call(functools.partial(step_kernel, n, nj, slots, heads, hd), o...  66.8 us
    pallas_call x1, Pallas kernels, store(): pl.pallas_call(functools.partial(store_kernel, blk, slots, heads, hd), ou...  13 us
    unnamed x1, local copies, waits for them, and re-layouts  2.02 us

profile of v2, /device:TPU:113, one launch (start us, length us, event | category | flops | bytes accessed | tf_op | source)
XLA Modules:
  0.0 82.6 jit_solution(12527461241546548751)
XLA Ops:
  0.6 66.8 %decode_step.1 = (bf16[65536,128]{1,0:T(8,128)(2,1)S(1)}, bf16[65536,128]{1,0:T(8,128)(2,1)S(1)}, bf16[1024,2048]{1,0:T(8,128)(2,1)S(1)}, f32[2,1024,128]{2,1,0:T(8,128)}, f32[2,1024,128]{2,1,0:T(8,128)}) custom-call(s32[8,128]{1,0:T(8,128)} %bitcast.10, bf16[128,256]{1,0:T(8,128)(2,1)} %constant.2.clone.tab_ref, f32[1,256]{1,0:T(1,128)} %bitcast.12, ...), custom_call_target="tpu_custom_call" | custom-call | tf_op jit(solution)/shard_map/decode_step/pallas_call | solution.py:361
  67.4 2.0 %copy.20 = bf16[1024,2048]{1,0:T(8,128)(2,1)} copy(bf16[1024,2048]{1,0:T(8,128)(2,1)S(1)} %get-tuple-element.17) | data formatting | bytes 8388608
  69.4 13.0 %store.1 = (bf16[65536,128]{1,0:T(8,128)(2,1)}, bf16[65536,128]{1,0:T(8,128)(2,1)}, bf16[65536,128]{1,0:T(8,128)(2,1)S(1)}, bf16[65536,128]{1,0:T(8,128)(2,1)S(1)}) custom-call(s32[1024]{0:T(1024)} %pos_s.1, f32[2,1024,128]{2,1,0:T(8,128)} %get-tuple-element.11.kn, ...), custom_call_target="tpu_custom_call", output_to_operand_aliasing={{2}: (3, {}), {3}: (4, {})} | custom-call | tf_op jit(solution)/shard_map/store/pallas_call | solution.py:422

commit v3 on v2

--- a/solution.py
+++ b/solution.py
@@ -16,7 +16,14 @@
 VMEM_SPEC = pl.BlockSpec(memory_space=pltpu.VMEM)
 HBM_SPEC = pl.BlockSpec(memory_space=pltpu.HBM)
 LANES = 128
-BLK = 64
+BLK = 128
+CHUNKS = (2, 2, 2, 2)
+ORDER = (
+         'Q0', 'Q1', 'R0', 'T0.0', 'T0.1', 'a0', 'R1', 'b0', 'T1.0', 'T1.1', 'a1', 'Q2',
+         'c0', 'b1', 'Q3', 'R2', 'T2.0', 'd0', 'T2.1', 'c1', 'a2', 'R3', 'b2', 'T3.0',
+         'T3.1', 'e0', 'a3', 'b3', 'c2', 'f0', 'd1', 'c3', 'd2', 'e1', 'd3', 'e2',
+         'e3', 'f1', 'f2', 'f3',
+)
 
 
 def rope_table(slots, head_dim):
@@ -34,42 +41,45 @@
     return np.concatenate(parts + [pad], axis=0)
 
 
-O, A_R, A_L, B_R, B_L, C_R, C_L, G1_R, G1_L, G2_R, G2_L, D_OWN, D_LEFT, D_RIGHT, D_ANT0, D_ANT1 = range(16)
-
-
-def step_kernel(n, nj, slots, heads, hd,
-                pos_ref, tab_ref, qw_ref, kw_ref, pw_ref, hid_hbm, wq_hbm, wk_hbm, wv_hbm, wo_hbm, kc_hbm, vc_hbm,
+(O, A_R, A_L, B_R, B_L, C_R, C_L, G1_R0, G1_R1, G1_L0, G1_L1, G2_R, G2_L,
+ D_OWN, D_LEFT, D_RIGHT, D_ANT0, D_ANT1) = range(18)
+
+
+def step_kernel(n, sizes, slots, heads, hd,
+                pos_hbm, tab_hbm, qw_hbm, kw_hbm, pw_hbm, hid_hbm, wq_hbm, wk_hbm, wv_hbm, wo_hbm, kc_hbm, vc_hbm,
                 kc, vc, out_ref, kn_hbm, vn_hbm,
-                kn, vn, hid, wq, wk, wv, wo, wop, qf, kf, qg, pcol, s_scr, p_scr, o_scr, opart, part, ra, rb, rc, cst,
-                esend, erecv, lsem, csem, nsem, osem, essem, ersem, ssem, rsem):
+                kn, vn, pos_ref, tab_ref, qw_ref, kw_ref, pw_ref, hid, wq, wk, wv, wo, wop, qf, kf, qg, pcol, s_scr, p_scr, o_scr, opart, part, ra, rb, rc, cst,
+                esend, erecv, lsem, psem, csem, nsem, osem, essem, ersem, ssem, rsem):
     me = lax.axis_index('tp')
     rows, width = hid_hbm.shape
     cols = heads * hd
     per_row = slots * heads
-    rc_rows = rows // nj
-    per = rc_rows // LANES
+    nj = len(sizes)
+    starts = [sum(sizes[:j]) for j in range(nj)]
     nchip = n // 2
     chip, core = me // 2, lax.rem(me, 2)
-    half_rows = rc_rows // 2
-    own = half_rows // nchip
-    hf = own // 2
+    half_of = [r // 2 for r in sizes]
+    own_of = [r // n for r in sizes]
+    hf_of = [r // (2 * n) for r in sizes]
     xr, xl, xa = lax.rem(chip + 1, nchip), lax.rem(chip + nchip - 1, nchip), lax.rem(chip + 2, nchip)
     right, left, mate = xr * 2 + core, xl * 2 + core, chip * 2 + (1 - core)
     f32, bf16 = jnp.float32, jnp.bfloat16
 
     def chunk(c):
-        return pl.ds(c * rc_rows, rc_rows)
+        return pl.ds(starts[c], sizes[c])
 
     ld_w = [pltpu.make_async_copy(src, dst, lsem.at[k]) for k, (src, dst) in
             enumerate(((wq_hbm, wq), (wk_hbm, wk), (wv_hbm, wv), (wo_hbm, wo)))]
     ld_h = [pltpu.make_async_copy(hid_hbm.at[chunk(c)], hid.at[chunk(c)], lsem.at[4 + c]) for c in range(nj)]
 
     def ld_kv(c):
-        sl = pl.ds(c * rc_rows * per_row, rc_rows * per_row)
+        sl = pl.ds(starts[c] * per_row, sizes[c] * per_row)
         return [pltpu.make_async_copy(kc_hbm.at[sl], kc.at[sl], csem.at[0, c]),
                 pltpu.make_async_copy(vc_hbm.at[sl], vc.at[sl], csem.at[1, c])]
 
-    for cp in (ld_h[0], ld_w[0], ld_w[1], ld_w[2], ld_h[1]):
+    ld_p = [pltpu.make_async_copy(src, dst, psem.at[k]) for k, (src, dst) in enumerate(
+        ((pos_hbm, pos_ref), (tab_hbm, tab_ref), (qw_hbm, qw_ref), (kw_hbm, kw_ref), (pw_hbm, pw_ref)))]
+    for cp in [ld_h[0], ld_w[0], ld_w[1]] + ld_p + [ld_w[2], ld_h[1]]:
         cp.start()
 
     barrier = pltpu.get_barrier_semaphore()
@@ -102,7 +112,7 @@
         device_id={'tp': mate}, device_id_type=MESH)
 
     def project_qkv(c):
-        cs = chunk(c)
+        cs, per = chunk(c), sizes[c] // LANES
         ld_h[c].wait()
         rows_out = []
         for k, (w, f) in enumerate(((wq, qf), (wk, kf))):
@@ -113,6 +123,9 @@
             en = jnp.sum(val * val, axis=1, keepdims=True)
             for b in range(per):
                 rows_out.append(to_row(en[b * LANES:(b + 1) * LANES]))
+            if c == 0 and k == 1:
+                for cp in ld_h[2:4] + ld_kv(0) + ld_kv(1) + ld_h[4:] + [ld_w[3]]:
+                    cp.start()
         pad = 8 - len(rows_out)
         esend[c] = jnp.concatenate(rows_out + [jnp.zeros((pad, LANES), f32)], axis=0)
         if c == 0:
@@ -121,23 +134,27 @@
             energy_copy(c, d).start()
         if c == 0:
             ld_w[2].wait()
-            for cp in ld_kv(0) + ld_h[2:] + [ld_w[3]]:
+            wo_copy.start()
+        if 0 < c < nj - 1:
+            for cp in ld_kv(c + 1):
                 cp.start()
-            wo_copy.start()
         val = jnp.dot(hid[cs, :], wv[...], preferred_element_type=f32).astype(bf16).astype(f32)
         for h in range(heads):
             vn[h, cs, :] = val[:, h * hd:(h + 1) * hd]
 
     def norm_rope(c):
-        total = esend[c]
+        if c == 0:
+            for cp in ld_p:
+                cp.wait()
+        total, per = esend[c], sizes[c] // LANES
         for d in range(1, n):
             energy_copy(c, d).wait_recv()
             total = total + erecv[c, d - 1]
         inv = lax.rsqrt(total / width + NORM_EPS)
         for b in range(per):
-            base = c * rc_rows + b * LANES
+            base = starts[c] + b * LANES
             rs = pl.ds(base, LANES)
-            p = to_col(pos_ref[c * per + b:c * per + b + 1, :].astype(f32)).astype(jnp.int32)
+            p = to_col(pos_ref[starts[c] // LANES + b:starts[c] // LANES + b + 1, :].astype(f32)).astype(jnp.int32)
             pcol[rs, :] = jnp.broadcast_to(p, (LANES, LANES))
             hot = jnp.logical_and(lane < 3 * slots, lane % slots == p)
             trig = jnp.dot(jnp.where(hot, 1.0, 0.0).astype(bf16), tab_ref[...], preferred_element_type=f32)
@@ -195,22 +212,30 @@
                     [res[0][8 * h:8 * h + 8], res[1][8 * h:8 * h + 8]], axis=0).astype(bf16)
         return carry
 
-    blocks = rc_rows // BLK
-
-    def attend(c, first, count):
-        if first == 0:
+    def attend(c, piece):
+        if piece == 0:
             for cp in ld_kv(c):
                 cp.wait()
-            if c + 1 < nj:
-                for cp in ld_kv(c + 1):
-                    cp.start()
-        lax.fori_loop(c * blocks + first, c * blocks + first + count, attend_block, 0)
-
-    def qs(y, part_no, count):
-        return pl.ds(pl.multiple_of(y * own + part_no * hf, hf), count)
-
-    def gs(j, c, y, part_no, count):
-        return pl.ds(pl.multiple_of(j * rc_rows + c * half_rows + y * own + part_no * hf, hf), count)
+        first = (starts[c] + piece * LANES) // BLK
+        lax.fori_loop(first, first + LANES // BLK, attend_block, 0)
+
+    def mine_of(j):
+        return pl.ds(starts[j] // 2, half_of[j])
+
+    def fs(j):
+        return pl.ds(starts[j] // (2 * n), hf_of[j])
+
+    def qs(j, y, part_no):
+        return pl.ds(pl.multiple_of(starts[j] // 2 + y * own_of[j] + part_no * hf_of[j], hf_of[j]), hf_of[j])
+
+    def os(j, c):
+        return pl.ds(pl.multiple_of(starts[j] + c * half_of[j], half_of[j]), half_of[j])
+
+    def gs(j, c, y, part_no=None):
+        first = starts[j] + c * half_of[j] + y * own_of[j]
+        if part_no is None:
+            return pl.ds(pl.multiple_of(first, own_of[j]), own_of[j])
+        return pl.ds(pl.multiple_of(first + part_no * hf_of[j], hf_of[j]), hf_of[j])
 
     def remote(kind, j, src, dst, dev):
         return pltpu.make_async_remote_copy(src_ref=src, dst_ref=dst, send_sem=ssem.at[kind, j], recv_sem=rsem.at[kind, j],
@@ -227,117 +252,84 @@
         remote(kind, j, dst, dst, dev).wait_recv()
 
     def p0(j):
-        src = pl.ds(pl.multiple_of(j * rc_rows + (1 - core) * half_rows, half_rows), half_rows)
-        send(O, j, o_scr.at[src], opart.at[j], mate)
+        send(O, j, o_scr.at[os(j, 1 - core)], opart.at[mine_of(j)], mate)
 
     def p1(j):
         if j == 0:
             ld_w[3].wait()
             wo_copy.wait_recv()
-        recv(O, j, opart.at[j], mate)
-        mine = o_scr[pl.ds(pl.multiple_of(j * rc_rows + core * half_rows, half_rows), half_rows), :]
-        theirs = opart[j]
+        recv(O, j, opart.at[mine_of(j)], mate)
+        mine = o_scr[os(j, core), :]
+        theirs = opart[mine_of(j), :]
         step = 512
         for c0 in range(0, width, step):
             acc = jnp.dot(mine, wo[:, c0:c0 + step], preferred_element_type=f32)
             acc = acc + jnp.dot(theirs, wop[:, c0:c0 + step], preferred_element_type=f32)
-            part[j, :, c0:c0 + step] = acc.astype(bf16)
-        send(A_R, j, part.at[j, qs(xa, 0, hf)], ra.at[j, 0], right)
-        send(A_L, j, part.at[j, qs(xa, 1, hf)], ra.at[j, 1], left)
-        send(B_R, j, part.at[j, qs(xr, 1, hf)], rb.at[j, 0], right)
-        send(B_L, j, part.at[j, qs(xl, 0, hf)], rb.at[j, 1], left)
+            part[mine_of(j), c0:c0 + step] = acc.astype(bf16)
+        send(A_R, j, part.at[qs(j, xa, 0)], ra.at[0, fs(j)], right)
+        send(A_L, j, part.at[qs(j, xa, 1)], ra.at[1, fs(j)], left)
+        send(B_R, j, part.at[qs(j, xr, 1)], rb.at[0, fs(j)], right)
+        send(B_L, j, part.at[qs(j, xl, 0)], rb.at[1, fs(j)], left)
 
     def p2(j):
-        recv(A_R, j, ra.at[j, 0], left)
-        cst[j, 0] = (part[j, qs(xr, 0, hf), :].astype(f32) + ra[j, 0].astype(f32)).astype(bf16)
-        send(C_R, j, cst.at[j, 0], rc.at[j, 0], right)
-        recv(A_L, j, ra.at[j, 1], right)
-        cst[j, 1] = (part[j, qs(xl, 1, hf), :].astype(f32) + ra[j, 1].astype(f32)).astype(bf16)
-        send(C_L, j, cst.at[j, 1], rc.at[j, 1], left)
+        for k in range(2):
+            recv((A_R, A_L)[k], j, ra.at[k, fs(j)], (left, right)[k])
+            own_part = part[qs(j, (xr, xl)[k], k), :].astype(f32)
+            cst[k, fs(j), :] = (own_part + ra[k, fs(j), :].astype(f32)).astype(bf16)
+            send((C_R, C_L)[k], j, cst.at[k, fs(j)], rc.at[k, fs(j)], (right, left)[k])
 
     def p3(j):
         for k in range(2):
-            recv((C_R, C_L)[k], j, rc.at[j, k], (left, right)[k])
-            recv((B_L, B_R)[k], j, rb.at[j, 1 - k], (right, left)[k])
-            a = (part[j, qs(chip, k, hf), :].astype(f32) + rc[j, k].astype(f32) + rb[j, 1 - k].astype(f32))
+            recv((B_L, B_R)[k], j, rb.at[1 - k, fs(j)], (right, left)[k])
+            recv((C_R, C_L)[k], j, rc.at[k, fs(j)], (left, right)[k])
+            a = (part[qs(j, chip, k), :].astype(f32) + rc[k, fs(j), :].astype(f32) + rb[1 - k, fs(j), :].astype(f32))
             inv = lax.rsqrt(jnp.sum(a * a, axis=1, keepdims=True) / width + NORM_EPS)
-            mine = gs(j, core, chip, k, hf)
+            mine = gs(j, core, chip, k)
             out_ref[mine, :] = (hid[mine, :].astype(f32) + a * inv * pw_ref[...]).astype(bf16)
-        blk = out_ref.at[gs(j, core, chip, 0, own)]
-        send(G1_R, j, blk, blk, right)
-        send(G1_L, j, blk, blk, left)
+        blk = out_ref.at[gs(j, core, chip)]
+        h0, h1 = out_ref.at[gs(j, core, chip, 0)], out_ref.at[gs(j, core, chip, 1)]
+        send(G1_R0, j, h0, h0, right)
+        send(G1_L1, j, h1, h1, left)
+        send(G1_R1, j, h1, h1, right)
+        send(G1_L0, j, h0, h0, left)
         send(D_OWN, j, blk, blk, mate)
 
     def p4(j):
-        bl = out_ref.at[gs(j, core, xl, 0, own)]
-        br = out_ref.at[gs(j, core, xr, 0, own)]
-        recv(G1_R, j, bl, left)
-        fl = out_ref.at[gs(j, core, xl, 0, hf)]
-        send(G2_R, j, fl, fl, right)
-        send(D_LEFT, j, bl, bl, mate)
-        recv(G1_L, j, br, right)
-        fr = out_ref.at[gs(j, core, xr, 1, hf)]
-        send(G2_L, j, fr, fr, left)
-        send(D_RIGHT, j, br, br, mate)
+        bl = [out_ref.at[gs(j, core, xl, k)] for k in range(2)]
+        br = [out_ref.at[gs(j, core, xr, k)] for k in range(2)]
+        recv(G1_R0, j, bl[0], left)
+        send(G2_R, j, bl[0], bl[0], right)
+        recv(G1_L1, j, br[1], right)
+        send(G2_L, j, br[1], br[1], left)
+        recv(G1_R1, j, bl[1], left)
+        full_l = out_ref.at[gs(j, core, xl)]
+        send(D_LEFT, j, full_l, full_l, mate)
+        recv(G1_L0, j, br[0], right)
+        full_r = out_ref.at[gs(j, core, xr)]
+        send(D_RIGHT, j, full_r, full_r, mate)
 
     def p5(j):
-        b0 = out_ref.at[gs(j, core, xa, 0, hf)]
+        b0 = out_ref.at[gs(j, core, xa, 0)]
         recv(G2_R, j, b0, left)
         send(D_ANT0, j, b0, b0, mate)
-        b1 = out_ref.at[gs(j, core, xa, 1, hf)]
+        b1 = out_ref.at[gs(j, core, xa, 1)]
         recv(G2_L, j, b1, right)
         send(D_ANT1, j, b1, b1, mate)
 
     new_out = [pltpu.make_async_copy(kn, kn_hbm, nsem.at[0]), pltpu.make_async_copy(vn, vn_hbm, nsem.at[1])]
-    qh, kh = blocks // 2, blocks - blocks // 2
-    project_qkv(0)
-    project_qkv(1)
-    norm_rope(0)
-    attend(0, 0, blocks)
-    p0(0)
-    norm_rope(1)
-    p1(0)
-    attend(1, 0, qh)
-    p2(0)
-    attend(1, qh, kh)
-    p0(1)
-    project_qkv(2)
-    p1(1)
-    p3(0)
-    norm_rope(2)
-    attend(2, 0, qh)
-    p2(1)
-    p4(0)
-    attend(2, qh, kh)
-    p0(2)
-    project_qkv(3)
-    p1(2)
-    p3(1)
-    p5(0)
-    norm_rope(3)
-    for cp in new_out:
-        cp.start()
-    attend(3, 0, qh)
-    p2(2)
-    p4(1)
-    attend(3, qh, kh)
-    p0(3)
-    p1(3)
-    p3(2)
-    p5(1)
-    p2(3)
-    p4(2)
-    p3(3)
-    p5(2)
-    p4(3)
-    p5(3)
+    stages = dict(Q=project_qkv, R=norm_rope, T=attend, a=p0, b=p1, c=p2, d=p3, e=p4, f=p5)
+    for token in ORDER:
+        stages[token[0]](*map(int, token[1:].split('.')))
+        if token == 'R' + str(nj - 1):
+            for cp in new_out:
+                cp.start()
     for j in range(nj):
         oc = 1 - core
-        recv(D_OWN, j, out_ref.at[gs(j, oc, chip, 0, own)], mate)
-        recv(D_LEFT, j, out_ref.at[gs(j, oc, xl, 0, own)], mate)
-        recv(D_RIGHT, j, out_ref.at[gs(j, oc, xr, 0, own)], mate)
-        recv(D_ANT0, j, out_ref.at[gs(j, oc, xa, 0, hf)], mate)
-        recv(D_ANT1, j, out_ref.at[gs(j, oc, xa, 1, hf)], mate)
+        recv(D_OWN, j, out_ref.at[gs(j, oc, chip)], mate)
+        recv(D_LEFT, j, out_ref.at[gs(j, oc, xl)], mate)
+        recv(D_RIGHT, j, out_ref.at[gs(j, oc, xr)], mate)
+        recv(D_ANT0, j, out_ref.at[gs(j, oc, xa, 0)], mate)
+        recv(D_ANT1, j, out_ref.at[gs(j, oc, xa, 1)], mate)
     for cp in sent:
         cp.wait_send()
     for c in range(nj):
@@ -348,33 +340,32 @@
         cp.wait()
 
 
-def decode_step(n, slots, heads, hd, positions, hidden, w_q, w_k, w_v, w_o, q_norm_w, k_norm_w, post_norm_w, k_flat, v_flat, nj=4):
+def decode_step(n, slots, heads, hd, positions, hidden, w_q, w_k, w_v, w_o, q_norm_w, k_norm_w, post_norm_w, k_flat, v_flat, sizes):
     rows, width = hidden.shape
     cols = heads * hd
-    rc_rows = rows // nj
-    half = rc_rows // 2
-    own = half // (n // 2)
-    hf = own // 2
+    nj = len(sizes)
     span = 8 * slots * heads
     f32, bf16 = jnp.float32, jnp.bfloat16
     dma = pltpu.SemaphoreType.DMA
     return pl.pallas_call(
-        functools.partial(step_kernel, n, nj, slots, heads, hd),
+        functools.partial(step_kernel, n, sizes, slots, heads, hd),
         out_shape=(pltpu.VMEM(k_flat.shape, bf16), pltpu.VMEM(v_flat.shape, bf16), pltpu.VMEM((rows, width), bf16),
                    jax.ShapeDtypeStruct((heads, rows, hd), f32), jax.ShapeDtypeStruct((heads, rows, hd), f32)),
-        in_specs=[VMEM_SPEC] * 5 + [HBM_SPEC] * 7,
+        in_specs=[HBM_SPEC] * 12,
         out_specs=(VMEM_SPEC,) * 3 + (HBM_SPEC,) * 2,
         scratch_shapes=[
             pltpu.VMEM((heads, rows, hd), f32), pltpu.VMEM((heads, rows, hd), f32),
+            pltpu.VMEM((rows // LANES, LANES), jnp.int32), pltpu.VMEM((LANES, 2 * hd), bf16), pltpu.VMEM((1, cols), f32),
+            pltpu.VMEM((1, cols), f32), pltpu.VMEM((1, width), f32),
             pltpu.VMEM((rows, width), bf16), pltpu.VMEM((width, cols), bf16), pltpu.VMEM((width, cols), bf16),
             pltpu.VMEM((width, cols), bf16), pltpu.VMEM((cols, width), bf16), pltpu.VMEM((cols, width), bf16),
             pltpu.VMEM((rows, cols), f32), pltpu.VMEM((rows, cols), f32), pltpu.VMEM((rows // 8, 8 * heads, hd), bf16),
             pltpu.VMEM((rows, LANES), jnp.int32), pltpu.VMEM((BLK * heads, span), f32), pltpu.VMEM((BLK * heads, span), bf16),
-            pltpu.VMEM((rows, cols), bf16), pltpu.VMEM((nj, half, cols), bf16), pltpu.VMEM((nj, half, width), bf16),
-            pltpu.VMEM((nj, 2, hf, width), bf16), pltpu.VMEM((nj, 2, hf, width), bf16),
-            pltpu.VMEM((nj, 2, hf, width), bf16), pltpu.VMEM((nj, 2, hf, width), bf16),
+            pltpu.VMEM((rows, cols), bf16), pltpu.VMEM((rows // 2, cols), bf16), pltpu.VMEM((rows // 2, width), bf16),
+            pltpu.VMEM((2, rows // (2 * n), width), bf16), pltpu.VMEM((2, rows // (2 * n), width), bf16),
+            pltpu.VMEM((2, rows // (2 * n), width), bf16), pltpu.VMEM((2, rows // (2 * n), width), bf16),
             pltpu.VMEM((nj, 8, LANES), f32), pltpu.VMEM((nj, n - 1, 8, LANES), f32),
-            dma((4 + nj,)), dma((2, nj)), dma((2,)), dma((2,)), dma((nj, n - 1)), dma((nj, n - 1)), dma((16, nj)), dma((16, nj)),
+            dma((4 + nj,)), dma((5,)), dma((2, nj)), dma((2,)), dma((2,)), dma((nj, n - 1)), dma((nj, n - 1)), dma((18, nj)), dma((18, nj)),
         ],
         compiler_params=pltpu.CompilerParams(collective_id=0, has_side_effects=True, vmem_limit_bytes=26 << 20),
         name='decode_step',
@@ -433,6 +424,11 @@
     return res[:2]
 
 
+def chunk_sizes(rows):
+    unit = rows // 8
+    return [unit * k for k in CHUNKS]
+
+
 def solution(mesh):
     n = mesh.shape['tp']
 
@@ -440,7 +436,7 @@
         rows, slots, heads, hd = k_cache.shape
         flat = (rows * slots * heads, hd)
         k_vm, v_vm, hid_vm, kn, vn = decode_step(n, slots, heads, hd, positions, hidden, w_q, w_k, w_v, w_o, q_norm_w,
-                                                 k_norm_w, post_norm_w, k_cache.reshape(flat), v_cache.reshape(flat))
+                                                 k_norm_w, post_norm_w, k_cache.reshape(flat), v_cache.reshape(flat), chunk_sizes(rows))
         k_new, v_new = store(positions, kn, vn, k_vm, v_vm, slots, heads, hd)
         return hid_vm, k_new.reshape(k_cache.shape), v_new.reshape(v_cache.shape)
 

time: 82.8 us -> 70 us (0.85)
  Pallas kernels: 79.8 us -> 67.1 us
    pallas_call x1, Pallas kernels: 66.8 us -> 54.1 us  [decode_step(): pl.pallas_call(functools.partial(step_kernel, n, sizes, slots, heads, hd)...]
where the time goes in v3:
time: 70 us; the launch traced here: 69.9 us
  Pallas kernels  67.1 us (96%)
  local copies, waits for them, and re-layouts  2.02 us (3%)
  between operations  0.8 us (1%)
    pallas_call x1, Pallas kernels, decode_step(): pl.pallas_call(functools.partial(step_kernel, n, sizes, slots, heads, hd)...  54.1 us
    pallas_call x1, Pallas kernels, store(): pl.pallas_call(functools.partial(store_kernel, blk, slots, heads, hd), ou...  13 us
    unnamed x1, local copies, waits for them, and re-layouts  2.02 us

profile of v3, /device:TPU:113, one launch (start us, length us, event | category | flops | bytes accessed | tf_op | source)
XLA Modules:
  0.0 69.9 jit_solution(5321469472144165651)
XLA Ops:
  0.6 54.1 %decode_step.1 = (bf16[65536,128]{1,0:T(8,128)(2,1)S(1)}, bf16[65536,128]{1,0:T(8,128)(2,1)S(1)}, bf16[1024,2048]{1,0:T(8,128)(2,1)S(1)}, f32[2,1024,128]{2,1,0:T(8,128)}, f32[2,1024,128]{2,1,0:T(8,128)}) custom-call(s32[8,128]{1,0:T(8,128)} %bitcast.10, bf16[128,256]{1,0:T(8,128)(2,1)} %constant.2.clone.tab_hbm, f32[1,256]{1,0:T(1,128)} %bitcast.12, ...), custom_call_target="tpu_custom_call" | custom-call | tf_op jit(solution)/shard_map/decode_step/pallas_call | solution.py:350
  54.7 2.0 %copy.20 = bf16[1024,2048]{1,0:T(8,128)(2,1)} copy(bf16[1024,2048]{1,0:T(8,128)(2,1)S(1)} %get-tuple-element.17) | data formatting | bytes 8388608
  56.8 13.0 %store.1 = (bf16[65536,128]{1,0:T(8,128)(2,1)}, bf16[65536,128]{1,0:T(8,128)(2,1)}, bf16[65536,128]{1,0:T(8,128)(2,1)S(1)}, bf16[65536,128]{1,0:T(8,128)(2,1)S(1)}) custom-call(s32[1024]{0:T(1024)} %pos_s.1, f32[2,1024,128]{2,1,0:T(8,128)} %get-tuple-element.11.kn, ...), custom_call_target="tpu_custom_call", output_to_operand_aliasing={{2}: (3, {}), {3}: (4, {})} | custom-call | tf_op jit(solution)/shard_map/store/pallas_call | solution.py:413

commit v4 on v3

--- a/solution.py
+++ b/solution.py
@@ -22,7 +22,7 @@
          'Q0', 'Q1', 'R0', 'T0.0', 'T0.1', 'a0', 'R1', 'b0', 'T1.0', 'T1.1', 'a1', 'Q2',
          'c0', 'b1', 'Q3', 'R2', 'T2.0', 'd0', 'T2.1', 'c1', 'a2', 'R3', 'b2', 'T3.0',
          'T3.1', 'e0', 'a3', 'b3', 'c2', 'f0', 'd1', 'c3', 'd2', 'e1', 'd3', 'e2',
-         'e3', 'f1', 'f2', 'f3',
+         'f1', 'e3', 'f2', 'f3',
 )
 
 

time: 70 us -> 70 us (level)
  no operation moved by 1% of the time
where the time goes in v4:
time: 70 us; the launch traced here: 69.9 us
  Pallas kernels  67.1 us (96%)
  local copies, waits for them, and re-layouts  2.02 us (3%)
  between operations  0.8 us (1%)
    pallas_call x1, Pallas kernels, decode_step(): pl.pallas_call(functools.partial(step_kernel, n, sizes, slots, heads, hd)...  54.1 us
    pallas_call x1, Pallas kernels, store(): pl.pallas_call(functools.partial(store_kernel, blk, slots, heads, hd), ou...  13 us
    unnamed x1, local copies, waits for them, and re-layouts  2.02 us

profile of v4, /device:TPU:113, one launch (start us, length us, event | category | flops | bytes accessed | tf_op | source)
XLA Modules:
  0.0 69.9 jit_solution(10377367025352856540)
XLA Ops:
  0.6 54.1 %decode_step.1 = (bf16[65536,128]{1,0:T(8,128)(2,1)S(1)}, bf16[65536,128]{1,0:T(8,128)(2,1)S(1)}, bf16[1024,2048]{1,0:T(8,128)(2,1)S(1)}, f32[2,1024,128]{2,1,0:T(8,128)}, f32[2,1024,128]{2,1,0:T(8,128)}) custom-call(s32[8,128]{1,0:T(8,128)} %bitcast.10, bf16[128,256]{1,0:T(8,128)(2,1)} %constant.2.clone.tab_hbm, f32[1,256]{1,0:T(1,128)} %bitcast.12, ...), custom_call_target="tpu_custom_call" | custom-call | tf_op jit(solution)/shard_map/decode_step/pallas_call | solution.py:350
  54.7 2.0 %copy.20 = bf16[1024,2048]{1,0:T(8,128)(2,1)} copy(bf16[1024,2048]{1,0:T(8,128)(2,1)S(1)} %get-tuple-element.17) | data formatting | bytes 8388608
  56.8 13.0 %store.1 = (bf16[65536,128]{1,0:T(8,128)(2,1)}, bf16[65536,128]{1,0:T(8,128)(2,1)}, bf16[65536,128]{1,0:T(8,128)(2,1)S(1)}, bf16[65536,128]{1,0:T(8,128)(2,1)S(1)}) custom-call(s32[1024]{0:T(1024)} %pos_s.1, f32[2,1024,128]{2,1,0:T(8,128)} %get-tuple-element.11.kn, ...), custom_call_target="tpu_custom_call", output_to_operand_aliasing={{2}: (3, {}), {3}: (4, {})} | custom-call | tf_op jit(solution)/shard_map/store/pallas_call | solution.py:413
